TPU v7x, 32 devices: a whole 2x2x4 slice. The times are simulated.
32 devices in a mesh: emit: 2 (over y), client: 16 (over z, x, core).
Axes of the slice: x: 2, y: 2, z: 4, core: 2. Of those that a mesh axis runs over, the one named last changes fastest.
Arguments:
- features: bfloat16 [65536, 768], P('client'), may hold values from -28 to 28
- labels: int32 [65536], P('client'), may hold values from 0 to 999
- client_ids: int32 [128], replicated, may hold values from 0 to 127, each once
- trunk_in: bfloat16 [128, 2048], replicated, may hold values from -6 to 6
- trunk_weight: bfloat16 [2048, 2048], P(None, 'client'), may hold values from -0.125 to 0.125
- class_table: bfloat16 [1000, 2048], P('emit'), may hold values from -6 to 6
- emit_weight: bfloat16 [2048, 768], P('emit'), may hold values from -0.125 to 0.125
Outputs:
- loss: float32 [65536], P('client')
- emit_grad: float32 [2048, 768], P(('emit', 'client'))
- trunk_grad: float32 [2048, 2048], P(None, ('emit', 'client'))
Inputs may be any that keep to these rules, and one draw needn't show every extreme that they name: Each client number appears once; slot s holds the features of client client_ids[s].
All inputs are finite; a program needn't handle non-finite values.
Results may differ from a plain program's by a relative error of at most 0.022.
Values may be sent and summed in bfloat16 or wider, within the bound.
No kernel may reach another device: no remote copies, remote signals or barrier semaphores. Data moves between devices by JAX's collectives and lax.ppermute only.
A program may use at most 128 MiB of HBM per device.

v0:
```python
import jax
import jax.numpy as jnp
from jax import lax
from jax.sharding import PartitionSpec as P

CL_DEV = 8


def silu_grad(value):
    sig = jax.nn.sigmoid(value)
    return sig * (1.0 + value * (1.0 - sig))


def per_device(features, labels, client_ids, trunk_in, trunk_weight, class_table, emit_weight):
    slots = CL_DEV
    clients = trunk_in.shape[0]
    hidden_dim = trunk_in.shape[1]
    classes = class_table.shape[0]
    feat_dim = features.shape[1]
    samples = features.shape[0] // slots
    client_index = lax.axis_index("client")
    emit_index = lax.axis_index("emit")
    pre_cols = jnp.dot(trunk_in, trunk_weight, preferred_element_type=jnp.float32).astype(
        jnp.bfloat16
    )
    pre_all = lax.all_gather(pre_cols, "client", axis=1, tiled=True)
    own_ids = lax.dynamic_slice_in_dim(client_ids, client_index * slots, slots)
    numbers = lax.iota(jnp.int32, clients)
    picker = (own_ids[:, None] == numbers[None, :]).astype(jnp.bfloat16)
    pre_own = jnp.dot(picker, pre_all, preferred_element_type=jnp.float32)
    code_in = jax.nn.silu(pre_own)[:, None, :] + class_table.astype(jnp.float32)[None, :, :]
    code = jax.nn.silu(code_in).astype(jnp.bfloat16).reshape(slots * classes, hidden_dim)
    emit_full = lax.all_gather(emit_weight, "emit", axis=0, tiled=True)
    heads = jnp.dot(code, emit_full, preferred_element_type=jnp.float32).astype(jnp.bfloat16)
    heads = heads.reshape(slots, classes, feat_dim)
    feats = features.reshape(slots, samples, feat_dim)
    logits = jnp.einsum("snd,skd->snk", feats, heads, preferred_element_type=jnp.float32)
    class_ids = emit_index * classes + lax.iota(jnp.int32, classes)
    onehot = (labels.reshape(slots, samples)[:, :, None] == class_ids[None, None, :]).astype(
        jnp.float32
    )
    target = jnp.sum(logits * onehot, axis=2)
    local_top = jnp.max(logits, axis=2)
    top = lax.pmax(local_top, "emit")
    expd = jnp.exp(logits - top[:, :, None])
    total, target_all = (
        lax.psum(jnp.sum(expd, axis=2).astype(jnp.bfloat16), "emit").astype(jnp.float32),
        lax.psum(target.astype(jnp.bfloat16), "emit").astype(jnp.float32),
    )
    loss = (top + jnp.log(total) - target_all).reshape(slots * samples)
    grad_logits = ((expd / total[:, :, None] - onehot) / clients).astype(jnp.bfloat16)
    grad_heads = jnp.einsum("snk,snd->skd", grad_logits, feats, preferred_element_type=jnp.float32)
    grad_heads = grad_heads.astype(jnp.bfloat16).reshape(slots * classes, feat_dim)
    partial_rows = lax.psum_scatter(
        jnp.einsum("rh,rd->hd", code, grad_heads, preferred_element_type=jnp.float32).astype(
            jnp.bfloat16
        ),
        "emit",
        scatter_dimension=0,
        tiled=True,
    )
    emit_grad = lax.psum_scatter(partial_rows, "client", scatter_dimension=0, tiled=True).astype(
        jnp.float32
    )
    grad_code = jnp.dot(grad_heads, emit_full.T, preferred_element_type=jnp.float32)
    grad_code = grad_code.reshape(slots, classes, hidden_dim)
    grad_sum = jnp.sum(grad_code * silu_grad(code_in), axis=1)
    block = hidden_dim // lax.axis_size("emit")
    grad_block = lax.psum_scatter(
        grad_sum.astype(jnp.bfloat16), "emit", scatter_dimension=1, tiled=True
    ).astype(jnp.float32)
    pre_block = lax.dynamic_slice_in_dim(pre_own, emit_index * block, block, 1)
    grad_pre = (grad_block * silu_grad(pre_block)).astype(jnp.bfloat16)
    grad_all = lax.all_gather(grad_pre, "client", axis=0, tiled=True)
    width = block // lax.axis_size("client")
    grad_mine = lax.dynamic_slice_in_dim(grad_all, client_index * width, width, 1)
    picker_all = (client_ids[:, None] == numbers[None, :]).astype(jnp.bfloat16)
    grad_client = jnp.einsum(
        "sc,sw->cw", picker_all, grad_mine, preferred_element_type=jnp.float32
    ).astype(jnp.bfloat16)
    trunk_grad = jnp.einsum("ch,cw->hw", trunk_in, grad_client, preferred_element_type=jnp.float32)
    return (loss, emit_grad, trunk_grad)


def solution(mesh):
    return jax.shard_map(
        per_device,
        mesh=mesh,
        in_specs=(
            P("client", None),
            P("client"),
            P(),
            P(),
            P(None, "client"),
            P("emit", None),
            P("emit", None),
        ),
        out_specs=(P("client"), P(("emit", "client"), None), P(None, ("emit", "client"))),
        check_vma=False,
    )
```

profile of v0, /device:TPU:0, one launch (start us, length us, event | category | flops | bytes accessed | tf_op | source)
XLA Modules:
  0.0 301.0 jit_solution(15818444923644420480)
XLA Ops:
  7.2 0.0 all-gather.2.cloned.1.call-start
  7.2 0.7 all-gather.2.cloned.1.call-update
  7.9 0.0 reduce-scatter.4.cloned.1.call-start
  8.0 4.1 %convert_element_type.57 = f32[500,2048]{1,0:T(8,128)} convert(bf16[500,2048]{1,0:T(8,128)(2,1)} %param.12) | non-fusion elementwise | flops 1024000 | bytes 6144000 | tf_op jit(solution)/shard_map/convert_element_type | solution.py:31
  12.1 0.7 dynamic_slice.9
  12.8 1.3 convolution_convert_fusion.1
  14.1 24.6 %all_gather.9 = bf16[128,2048]{1,0:T(8,128)(2,1)S(1)} all-gather(bf16[128,128]{1,0:T(8,128)(2,1)S(1)} %convolution_convert_fusion.1), channel_id=1, replica_groups=mesh['emit'=2,'client'=16] {'client'}, dimensions={1}, use_global_device_ids=true | all-gather | bytes 557056 | tf_op jit(solution)/shard_map/all_gather | solution.py:26
  38.7 0.9 divide_multiply_fusion
  39.6 12.5 %broadcast_add_fusion = f32[8,500,2048]{2,1,0:T(8,128)} fusion(f32[500,2048]{1,0:T(8,128)} %convert_element_type.57, f32[8,2048]{1,0:T(8,128)S(1)} %get-tuple-element.7), kind=kLoop, calls=%fused_computation.15 | loop fusion | flops 8192000 | bytes 36929536 | tf_op jit(solution)/shard_map/add | solution.py:31
  52.1 29.4 %add.75 = f32[4000,2048]{1,0:T(8,128)} reshape(f32[8,500,2048]{2,1,0:T(8,128)} %broadcast_add_fusion) | data formatting | bytes 65536000 | tf_op jit(solution)/shard_map/add | solution.py:31
  81.5 0.0 all-gather.2.cloned.1.call-done
  81.5 25.7 %fusion.20 = bf16[4000,768]{1,0:T(8,128)(2,1)} fusion(bf16[2048,768]{1,0:T(8,128)(2,1)} %all-gather.2.cloned.1.call-done, f32[4000,2048]{1,0:T(8,128)} %add.75), kind=kOutput, calls=%fused_computation.28 | convolution fusion | flops 12626944000 | bytes 42057728 | tf_op jit(solution)/shard_map/dot_general | solution.py:34
  107.2 6.3 %reshape.34 = bf16[8,500,768]{2,1,0:T(8,128)(2,1)} reshape(bf16[4000,768]{1,0:T(8,128)(2,1)} %fusion.20) | data formatting | bytes 12288000 | tf_op jit(solution)/shard_map/reshape | solution.py:35
  113.5 11.2 %bitcast_reduce_fusion = (f32[8,512]{1,0:T(8,128)S(1)}, f32[8,500,512]{2,1,0:T(8,128)}) fusion(bf16[8,500,768]{2,1,0:T(8,128)(2,1)} %reshape.34, bf16[8,512,768]{2,1,0:T(8,128)(2,1)} %bitcast.35), kind=kOutput, calls=%fused_computation.25 | convolution fusion | flops 3147771904 | bytes 20643840 | tf_op jit(solution)/shard_map/snd,skd->snk/dot_general | solution.py:37
  124.7 8.2 %pmax.7 = f32[8,512]{1,0:T(8,128)S(1)} all-reduce(f32[8,512]{1,0:T(8,128)S(1)} %get-tuple-element.9), channel_id=1, replica_groups=mesh['emit'=2,'client'=16] {'emit'}, use_global_device_ids=true, to_apply=%region_1.2 | all-reduce | flops 4096 | bytes 32768 | tf_op jit(solution)/shard_map/pmax | solution.py:44
  132.8 4.5 %fusion.19 = (bf16[8,512]{1,0:T(8,128)(2,1)S(1)}, bf16[8,512]{1,0:T(8,128)(2,1)S(1)}) fusion(f32[8,500,512]{2,1,0:T(8,128)} %get-tuple-element.10, f32[8,512]{1,0:T(8,128)S(1)} %pmax.7, s32[500]{0:T(512)S(1)} %iota_add_fusion, s32[8,512]{1,0:T(8,128)S(1)} %eq.44), kind=kLoop, calls=%fused_computation.27 | loop fusion | flops 10231808 | bytes 8243152 | tf_op jit(solution)/shard_map/reduce_sum | solution.py:47
  137.4 7.1 %all-reduce = (bf16[8,512]{1,0:T(8,128)(2,1)S(1)}, bf16[8,512]{1,0:T(8,128)(2,1)S(1)}) all-reduce(bf16[8,512]{1,0:T(8,128)(2,1)S(1)} %get-tuple-element.4, bf16[8,512]{1,0:T(8,128)(2,1)S(1)} %get-tuple-element.3), channel_id=1, replica_groups=mesh['emit'=2,'client'=16] {'emit'}, use_global_device_ids=true, to_apply=%region_5.6 | all-reduce | flops 8192 | bytes 32768 | tf_op jit(solution)/shard_map/psum | solution.py:48
  144.5 11.5 %fusion.30 = bf16[8,500,768]{2,1,0:T(8,128)(2,1)} fusion(bf16[8,512,768]{2,1,0:T(8,128)(2,1)} %bitcast.36, f32[8,500,512]{2,1,0:T(8,128)} %get-tuple-element.10, f32[8,512]{1,0:T(8,128)S(1)} %convert_element_type.61, s32[8,512]{1,0:T(8,128)S(1)} %eq.44, f32[8,512]{1,0:T(8,128)S(1)} %pmax.7, s32[500]{0:T(512)S(1)} %iota_add_fusion), kind=kOutput, calls=%fused_computation.36 | convolution fusion | flops 3163136000 | bytes 20678608 | tf_op jit(solution)/shard_map/snk,snd->skd/dot_general | solution.py:52
  156.0 20.2 %bitcast_convert_fusion = bf16[2048,768]{1,0:T(8,128)(2,1)} fusion(bf16[8,500,768]{2,1,0:T(8,128)(2,1)} %fusion.30, f32[500,2048]{1,0:T(8,128)S(1)} %copy-done.1, f32[8,2048]{1,0:T(8,128)S(1)} %get-tuple-element.7), kind=kOutput, calls=%fused_computation.29 | convolution fusion | flops 12633636864 | bytes 13451264 | tf_op jit(solution)/shard_map/rh,rd->hd/dot_general | solution.py:55
  176.2 0.0 reduce-scatter.4.cloned.1.call-update
  176.2 0.0 reduce-scatter.8.cloned.1.call-start
  176.3 24.4 %fusion.7 = bf16[8,2048]{1,0:T(8,128)(2,1)} fusion(bf16[8,500,768]{2,1,0:T(8,128)(2,1)} %fusion.30, f32[500,2048]{1,0:T(8,128)} %convert_element_type.57, f32[8,2048]{1,0:T(8,128)S(1)} %get-tuple-element.7, bf16[2048,768]{1,0:T(8,128)(2,1)} %all-gather.2.cloned.1.call-done), kind=kOutput, calls=%fused_computation.10 | convolution fusion | flops 12664815616 | bytes 13484032 | tf_op jit(solution)/shard_map/dot_general | solution.py:65
  200.7 0.0 reduce-scatter.8.cloned.1.call-update
  200.7 0.0 reduce-scatter.6.cloned.1.call-start
  200.8 16.3 %reduce-scatter.4.cloned.1.call-done = bf16[1024,768]{1,0:T(8,128)(2,1)} async-done(((bf16[2048,768]{1,0:T(8,128)(2,1)}), bf16[1024,768]{1,0:T(8,128)(2,1)}) %reduce-scatter.4.cloned.1.call-update) | async-done | bytes 1572880 | tf_op jit(solution)/shard_map/reduce_scatter | solution.py:54
  217.1 0.6 copy.10
  217.7 12.1 %reduce-scatter.8.cloned.1.call-done = bf16[8,1024]{1,0:T(8,128)(2,1)} async-done(((bf16[8,2048]{1,0:T(8,128)(2,1)}), bf16[8,1024]{1,0:T(8,128)(2,1)}) %reduce-scatter.8.cloned.1.call-update) | async-done | bytes 16400 | tf_op jit(solution)/shard_map/reduce_scatter | solution.py:69
  229.8 0.7 multiply_convert_fusion.4
  230.6 22.0 %all_gather.11 = bf16[128,1024]{1,0:T(8,128)(2,1)S(1)} all-gather(bf16[8,1024]{1,0:T(8,128)(2,1)S(1)} %multiply_convert_fusion.4), channel_id=1, replica_groups=mesh['emit'=2,'client'=16] {'client'}, dimensions={0}, use_global_device_ids=true | all-gather | bytes 278528 | tf_op jit(solution)/shard_map/all_gather | solution.py:74
  252.6 1.3 convolution_bitcast_fusion
  253.9 39.0 %reduce-scatter.6.cloned.1.call-done = bf16[64,768]{1,0:T(8,128)(2,1)} async-done(((bf16[1024,768]{1,0:T(8,128)(2,1)}), bf16[64,768]{1,0:T(8,128)(2,1)}) %reduce-scatter.6.cloned.1.call-update) | async-done | bytes 98320 | tf_op jit(solution)/shard_map/reduce_scatter | solution.py:62
  292.9 1.6 convert_element_type.69
  (15 shorter events, 0.1 us)
Async XLA Ops:
  7.2 5.6 %copy-start = (bf16[128,2048]{1,0:T(8,128)(2,1)S(1)}, bf16[128,2048]{1,0:T(8,128)(2,1)}, u32[]{:S(2)}) copy-start(bf16[128,2048]{1,0:T(8,128)(2,1)} %param.10) | copy-start | bytes 1572868
  7.2 74.3 %all-gather.2.cloned.1.call-start = ((), (), s32[]{:S(2)}) async-start(), calls=%async_computation.3 | async-start | bytes 4718592 | tf_op jit(solution)/shard_map/all_gather | solution.py:33
  7.9 209.2 %reduce-scatter.4.cloned.1.call-start = ((), (), s32[]{:S(2)}) async-start(), calls=%async_computation.4 | async-start | bytes 4718592 | tf_op jit(solution)/shard_map/reduce_scatter | solution.py:54
  52.1 29.4 %copy-start.3 = (s32[4096]{0:T(1024)S(1)}, s32[4096]{0:T(1024)}, u32[]{:S(2)}) copy-start(s32[4096]{0:T(1024)} %param.8) | copy-start | bytes 49156
  144.5 11.5 %copy-start.1 = (f32[500,2048]{1,0:T(8,128)S(1)}, f32[500,2048]{1,0:T(8,128)}, u32[]{:S(2)}) copy-start(f32[500,2048]{1,0:T(8,128)} %convert_element_type.57) | copy-start | bytes 12288004
  176.2 53.6 %copy-start.2 = (f32[8,2048]{1,0:T(8,128)S(1)}, f32[8,2048]{1,0:T(8,128)}, u32[]{:S(2)}) copy-start(f32[8,2048]{1,0:T(8,128)} %get-tuple-element.8) | copy-start | bytes 196612
  176.2 76.4 %copy-start.4 = (s32[128]{0:T(128)S(1)}, s32[128]{0:T(128)}, u32[]{:S(2)}) copy-start(s32[128]{0:T(128)} %param.9) | copy-start | bytes 1540
  176.2 53.6 %reduce-scatter.8.cloned.1.call-start = ((), (), s32[]{:S(2)}) async-start(), calls=%async_computation.6 | async-start | bytes 49152 | tf_op jit(solution)/shard_map/reduce_scatter | solution.py:69
  200.7 92.2 %reduce-scatter.6.cloned.1.call-start = ((), (), s32[]{:S(2)}) async-start(), calls=%async_computation.5 | async-start | bytes 1671168 | tf_op jit(solution)/shard_map/reduce_scatter | solution.py:62
Sparse Core Ops, SparseCore 0:
  9.5 47.6 all-gather.1
  176.3 40.7 reduce-scatter.3
  219.8 9.9 reduce-scatter.7
  233.3 59.5 reduce-scatter.5
where the time goes:
time: 302 us; the launch traced here: 301 us
  matrix products  96.5 us (32%)
  waiting for transfers between devices  68.1 us (23%)
  blocking collectives  61.9 us (20%)
  local copies, waits for them, and re-layouts  37.1 us (12%)
  other arithmetic  23.4 us (8%)
  between operations  13.8 us (5%)
    reduce_scatter x1, waiting for transfers between devices, per_device(): lax.psum_scatter(partial_rows, 'client', scatter_dimension=0, tiled=True)  39 us
    add x1, local copies, waits for them, and re-layouts, per_device(): jax.nn.silu(pre_own)[:, None, :]  29.4 us
    dot_general x1, matrix products, per_device(): jnp.dot(code, emit_full, preferred_element_type=jnp.float32)  25.7 us
    all_gather x1, blocking collectives, per_device(): pre_all = lax.all_gather(pre_cols, 'client', axis=1, tiled=True)  24.6 us
    dot_general x1, matrix products, per_device(): jnp.dot(grad_heads, emit_full.T, preferred_element_type=jnp.float32)  24.4 us
    all_gather x1, blocking collectives, per_device(): grad_all = lax.all_gather(grad_pre, 'client', axis=0, tiled=True)  22 us
    dot_general x1, matrix products, per_device(): jnp.einsum('rh,rd->hd', code, grad_heads, preferred_element_type=jnp.floa...  20.2 us
    reduce_scatter x1, waiting for transfers between devices, per_device(): lax.psum_scatter(jnp.einsum('rh,rd->hd', code, grad_heads, preferred_elem...  16.3 us
  transfers between devices with their start and end apart: 4, of which 3 were waited for; matrix products, arithmetic and copies ran while one was open for 25% of the time, Pallas kernels for 0%

commit v1 on v0

v1 whole, which is shorter than its diff:
```python
import functools

import jax
import jax.numpy as jnp
from jax import lax
from jax.experimental import pallas as pl
from jax.experimental.pallas import tpu as pltpu
from jax.sharding import PartitionSpec as P

MIB = 1024 * 1024


def params(mib):
    return pltpu.CompilerParams(vmem_limit_bytes=mib * MIB)


def matmul_cost(m, k, n, nbytes):
    return pl.CostEstimate(flops=2 * m * k * n, bytes_accessed=nbytes, transcendentals=0)


def silu_grad(value):
    sig = jax.nn.sigmoid(value)
    return sig * (1.0 + value * (1.0 - sig))


def code_kernel(classes, act_ref, table_ref, code_ref, slope_ref, half_ref):
    @pl.when(pl.program_id(0) == 0)
    def _():
        number = lax.broadcasted_iota(jnp.int32, half_ref.shape, 0)
        half = 0.5 * table_ref[...].astype(jnp.float32)
        half_ref[...] = jnp.where(number < classes, half, 0.0)

    y = act_ref[0] + half_ref[...]
    th = jnp.tanh(y)
    up = 1.0 + th
    code_ref[...] = (y * up).astype(jnp.bfloat16)
    slope_ref[...] = (up * (1.0 + y * (1.0 - th))).astype(jnp.bfloat16)


def forward_kernel(classes, where_ref, code_ref, local_ref, mine_ref, theirs_ref, feat_ref, label_ref, p_ref, stat_ref, emit_ref, heads_ref):
    rows, samples = p_ref.shape

    @pl.when(pl.program_id(0) == 0)
    def _():
        size = local_ref.shape[0]
        half = size // 2
        emit_index, core = where_ref[0], where_ref[1]
        emit_ref[pl.ds(pl.multiple_of(emit_index * size, size), size), :] = local_ref[...]
        for j in range(mine_ref.shape[0]):
            base = (emit_index ^ (j + 1)) * size
            first = pl.multiple_of(base + core * half, half)
            second = pl.multiple_of(base + (1 - core) * half, half)
            emit_ref[pl.ds(first, half), :] = mine_ref[j]
            emit_ref[pl.ds(second, half), :] = theirs_ref[j]

    step, last = pl.program_id(0), pl.num_programs(0) - 1

    def make_heads():
        return jnp.dot(
            code_ref[...], emit_ref[...], preferred_element_type=jnp.float32
        ).astype(jnp.bfloat16)

    def make_logits():
        return lax.dot_general(
            heads_ref[...], feat_ref[...], (((1,), (1,)), ((), ())),
            preferred_element_type=jnp.float32,
        )

    def soften(logits):
        number = lax.broadcasted_iota(jnp.int32, (rows, samples), 0)
        target = jnp.sum(jnp.where(number == label_ref[0], logits, 0.0), axis=0, keepdims=True)
        logits = jnp.where(number < classes, logits, -jnp.inf)
        top = jnp.max(logits, axis=0, keepdims=True)
        p = jnp.exp(logits - top)
        p_ref[...] = p
        stat_ref[0, 0:1, :] = top
        stat_ref[0, 1:2, :] = jnp.sum(p, axis=0, keepdims=True)
        stat_ref[0, 2:3, :] = target

    @pl.when(step == 0)
    def _():
        heads_ref[...] = make_heads()

    @pl.when((step > 0) & (step < last))
    def _():
        logits = make_logits()
        heads = make_heads()
        soften(logits)
        heads_ref[...] = heads

    @pl.when(step == last)
    def _():
        soften(make_logits())


def store_emit_grad(block, is_first, code, gh, keep_ref, send_ref):
    acc = lax.dot_general(code, gh, (((0,), (0,)), ((), ())), preferred_element_type=jnp.float32)
    width, feat_dim = acc.shape
    acc = acc.reshape(width // (2 * block), 2, block, feat_dim)
    first, second = acc[:, 0].reshape(width // 2, feat_dim), acc[:, 1].reshape(width // 2, feat_dim)
    keep_ref[...] = jnp.where(is_first, first, second).astype(jnp.bfloat16)
    send_ref[...] = jnp.where(is_first, second, first).astype(jnp.bfloat16)


def head_grad_kernel(inv_clients, block, slots, where_ref, p_ref, scale_ref, label_ref, feat_ref, code_ref, gh_ref, keep_ref, send_ref, all_ref):
    step = pl.program_id(0)
    rows = p_ref.shape[0]

    @pl.when(step < slots)
    def _():
        number = lax.broadcasted_iota(jnp.int32, p_ref.shape, 0)
        soft = p_ref[...] * scale_ref[0]
        grad = (soft - jnp.where(number == label_ref[0], 1.0, 0.0)) * inv_clients
        gh = jnp.dot(
            grad.astype(jnp.bfloat16), feat_ref[...], preferred_element_type=jnp.float32
        ).astype(jnp.bfloat16)
        gh_ref[...] = gh
        all_ref[pl.ds(pl.multiple_of(step * rows, rows), rows), :] = gh

    @pl.when(step >= slots)
    def _():
        store_emit_grad(block, where_ref[1] == 0, code_ref[...], all_ref[...], keep_ref, send_ref)


def store_code_grad(gh, slope_ref, emit_ref, pre_slope_ref, out_ref):
    hidden = emit_ref.shape[0]
    width = min(512, hidden)
    for c in range(hidden // width):
        cols = slice(c * width, (c + 1) * width)
        grad_code = lax.dot_general(
            gh, emit_ref[cols, :], (((1,), (1,)), ((), ())), preferred_element_type=jnp.float32
        )
        slope = slope_ref[:, cols].astype(jnp.float32)
        grad_sum = 0.5 * jnp.sum(grad_code * slope, axis=0, keepdims=True)
        out_ref[0, :, cols] = (grad_sum * pre_slope_ref[0, :, cols]).astype(out_ref.dtype)


def code_grad_kernel(slope_ref, emit_ref, pre_slope_ref, gh_ref, out_ref):
    store_code_grad(gh_ref[...], slope_ref, emit_ref, pre_slope_ref, out_ref)


def both_grads_kernel(block, count, slots, where_ref, slope_ref, emit_ref, pre_slope_ref, gh_ref, code_ref, out_ref, keep_ref, send_ref, all_ref):
    step = pl.program_id(0)
    rows = slope_ref.shape[0]

    @pl.when(step < count)
    def _():
        store_code_grad(gh_ref[...], slope_ref, emit_ref, pre_slope_ref, out_ref)

    @pl.when(step < slots)
    def _():
        all_ref[pl.ds(pl.multiple_of(step * rows, rows), rows), :] = gh_ref[...]

    @pl.when(step >= slots)
    def _():
        store_emit_grad(block, where_ref[1] == 0, code_ref[...], all_ref[...], keep_ref, send_ref)


def xor_pairs(size, bit):
    return [(i, i ^ bit) for i in range(size)]


def bits_of(size):
    return [1 << b for b in range(size.bit_length() - 1)]


def gather_emit(local, client_index):
    emits, clients = lax.axis_size("emit"), lax.axis_size("client")
    core = client_index & 1
    half = local.shape[0] // 2
    mine = lax.dynamic_slice_in_dim(local, core * half, half)[None]
    for bit in bits_of(emits):
        mine = jnp.concatenate([mine, lax.ppermute(mine, "emit", xor_pairs(emits, bit))])
    theirs = lax.ppermute(mine[1:], "client", xor_pairs(clients, 1))
    return mine[1:], theirs


def halve(value, dim, axis, size, bit, index):
    own = jnp.where((index & bit) != 0, 1, 0)
    send = lax.dynamic_index_in_dim(value, 1 - own, dim, keepdims=False)
    keep = lax.dynamic_index_in_dim(value, own, dim, keepdims=False)
    got = lax.ppermute(send, axis, xor_pairs(size, bit))
    return (keep.astype(jnp.float32) + got.astype(jnp.float32)).astype(jnp.bfloat16)


def per_device(features, labels, client_ids, trunk_in, trunk_weight, class_table, emit_weight):
    emits, client_size = lax.axis_size("emit"), lax.axis_size("client")
    clients, hidden = trunk_in.shape
    slots = clients // client_size
    classes = class_table.shape[0]
    feat_dim = features.shape[1]
    samples = features.shape[0] // slots
    rows = -(-classes // 128) * 128
    client_index = lax.axis_index("client")
    emit_index = lax.axis_index("emit")
    f32, bf16 = jnp.float32, jnp.bfloat16

    where = jnp.stack([emit_index, client_index & 1, emit_index // (emits // 2)]).astype(jnp.int32)
    pre_cols = jnp.dot(trunk_in, trunk_weight, preferred_element_type=f32).astype(bf16)
    numbers = lax.iota(jnp.int32, clients)
    picker = (client_ids[:, None] == numbers[None, :]).astype(bf16)
    pre_slots = jnp.dot(picker, pre_cols, preferred_element_type=f32).astype(bf16)
    pre_slots, emit_source = lax.optimization_barrier((pre_slots, emit_weight))
    pre_own = lax.all_to_all(
        pre_slots.reshape(client_size, slots, hidden // client_size), "client", 0, 0
    )
    pre_own = pre_own.transpose(1, 0, 2).reshape(slots, hidden).astype(f32)
    mine, theirs = gather_emit(emit_source, client_index)
    act = (0.5 * jax.nn.silu(pre_own))[:, None, :]
    pre_slope = silu_grad(pre_own)[:, None, :]
    local = labels - emit_index * classes
    local = jnp.where((local >= 0) & (local < classes), local, -1).reshape(slots, 1, samples)

    half = emit_weight.shape[0] // 2
    before = lambda s: jnp.maximum(s - 1, 0)
    once = dict(pipeline_mode=pl.Buffered(1))
    whole = lambda shape: pl.BlockSpec(shape, lambda s, *_: (0,) * len(shape), **once)
    per_slot = lambda shape: pl.BlockSpec((1,) + shape, lambda s, *_: (s, 0, 0))
    row_block = lambda shape: pl.BlockSpec(shape, lambda s, *_: (s, 0))
    make_code = pl.pallas_call(
        functools.partial(code_kernel, classes),
        grid=(slots,),
        in_specs=[per_slot((1, hidden)), whole((rows, hidden))],
        out_specs=[row_block((rows, hidden)), row_block((rows, hidden))],
        out_shape=[pltpu.HBM((slots * rows, hidden), bf16)] * 2,
        scratch_shapes=[pltpu.VMEM((rows, hidden), f32)],
        compiler_params=params(58),
        cost_estimate=pl.CostEstimate(
            flops=int(4e9), bytes_accessed=4 * slots * rows * hidden, transcendentals=0
        ),
        name="code",
    )
    code, slope = make_code(act, class_table)

    p, stats, emit_full = pl.pallas_call(
        functools.partial(forward_kernel, classes),
        grid_spec=pltpu.PrefetchScalarGridSpec(
            num_scalar_prefetch=1,
            grid=(slots + 1,),
            in_specs=[
                pl.BlockSpec((rows, hidden), lambda s, *_: (jnp.minimum(s, slots - 1), 0)),
                whole(emit_weight.shape),
                whole((emits - 1, half, feat_dim)),
                whole((emits - 1, half, feat_dim)),
                pl.BlockSpec((samples, feat_dim), lambda s, *_: (before(s), 0)),
                pl.BlockSpec((1, 1, samples), lambda s, *_: (before(s), 0, 0)),
            ],
            out_specs=[
                pl.BlockSpec((rows, samples), lambda s, *_: (before(s), 0)),
                pl.BlockSpec((1, 3, samples), lambda s, *_: (before(s), 0, 0)),
                pl.BlockSpec((hidden, feat_dim), lambda s, *_: (0, 0)),
            ],
            scratch_shapes=[pltpu.VMEM((rows, feat_dim), bf16)],
        ),
        out_shape=[
            jax.ShapeDtypeStruct((slots * rows, samples), f32),
            pltpu.HBM((slots, 3, samples), f32),
            pltpu.HBM((hidden, feat_dim), bf16),
        ],
        compiler_params=params(58),
        cost_estimate=matmul_cost(slots * rows, hidden + samples, feat_dim, 30 * MIB),
        name="forward",
    )(where, code, emit_weight, mine, theirs, features, local)

    top, total, target = stats[:, 0], stats[:, 1], stats[:, 2]
    for bit in bits_of(emits):
        other = lax.ppermute(jnp.stack([top, total, target], 1), "emit", xor_pairs(emits, bit))
        new_top = jnp.maximum(top, other[:, 0])
        total = total * jnp.exp(top - new_top) + other[:, 1] * jnp.exp(other[:, 0] - new_top)
        target = target + other[:, 2]
        top = new_top
    loss = (top + jnp.log(total) - target).reshape(slots * samples)
    scale = (jnp.exp(stats[:, 0] - top) / total)[:, None, :]

    block = hidden // (emits * client_size)
    width = min(256, hidden // 2)
    steps = hidden // 2 // width
    halves = [jax.ShapeDtypeStruct((hidden // 4, feat_dim), bf16)] * 2
    at = lambda bit: jnp.stack([bit * steps, where[1]]).astype(jnp.int32)
    slot_of = lambda s: jnp.minimum(s, slots - 1)
    step_of = lambda s: jnp.maximum(s - slots, 0)

    gh, keep_a, send_a = pl.pallas_call(
        functools.partial(head_grad_kernel, 1.0 / clients, block, slots),
        grid_spec=pltpu.PrefetchScalarGridSpec(
            num_scalar_prefetch=1,
            grid=(slots + steps,),
            in_specs=[
                pl.BlockSpec((rows, samples), lambda s, w: (slot_of(s), 0)),
                pl.BlockSpec((1, 1, samples), lambda s, w: (slot_of(s), 0, 0)),
                pl.BlockSpec((1, 1, samples), lambda s, w: (slot_of(s), 0, 0)),
                pl.BlockSpec((samples, feat_dim), lambda s, w: (slot_of(s), 0)),
                pl.BlockSpec((slots * rows, width), lambda s, w: (0, w[0] + step_of(s))),
            ],
            out_specs=[pl.BlockSpec((rows, feat_dim), lambda s, w: (slot_of(s), 0))]
            + [pl.BlockSpec((width // 2, feat_dim), lambda s, w: (step_of(s), 0))] * 2,
            scratch_shapes=[pltpu.VMEM((slots * rows, feat_dim), bf16)],
        ),
        out_shape=[pltpu.HBM((slots * rows, feat_dim), bf16)] + halves,
        compiler_params=params(58),
        cost_estimate=matmul_cost(feat_dim, slots * rows, hidden // 2 + samples, 20 * MIB),
        name="head_grad",
    )(at(1 - where[2]), p, scale, local, features, code)

    def both_grads(count, gh, code):
        early_of = lambda s: jnp.minimum(s, count - 1)
        return pl.pallas_call(
            functools.partial(both_grads_kernel, block, count, slots),
            grid_spec=pltpu.PrefetchScalarGridSpec(
                num_scalar_prefetch=1,
                grid=(slots + steps,),
                in_specs=[
                    pl.BlockSpec((rows, hidden), lambda s, w: (early_of(s), 0)),
                    whole((hidden, feat_dim)),
                    pl.BlockSpec((1, 1, hidden), lambda s, w: (early_of(s), 0, 0)),
                    pl.BlockSpec((rows, feat_dim), lambda s, w: (slot_of(s), 0)),
                    pl.BlockSpec((slots * rows, width), lambda s, w: (0, w[0] + step_of(s))),
                ],
                out_specs=[pl.BlockSpec((1, 1, hidden), lambda s, w: (early_of(s), 0, 0))]
                + [pl.BlockSpec((width // 2, feat_dim), lambda s, w: (step_of(s), 0))] * 2,
                scratch_shapes=[pltpu.VMEM((slots * rows, feat_dim), bf16)],
            ),
            out_shape=[jax.ShapeDtypeStruct((count, 1, hidden), bf16)] + halves,
            compiler_params=params(58),
            cost_estimate=matmul_cost(
                feat_dim, slots * rows, hidden // 2 + hidden * count // slots, 30 * MIB
            ),
            name="both_grads",
        )(at(where[2]), slope, emit_full, pre_slope, gh, code)

    def code_grad(first, count, gh):
        return pl.pallas_call(
            code_grad_kernel,
            grid=(count,),
            in_specs=[
                pl.BlockSpec((rows, hidden), lambda s: (s + first, 0)),
                whole((hidden, feat_dim)),
                pl.BlockSpec((1, 1, hidden), lambda s: (s + first, 0, 0)),
                pl.BlockSpec((rows, feat_dim), lambda s: (s + first, 0)),
            ],
            out_specs=per_slot((1, hidden)),
            out_shape=jax.ShapeDtypeStruct((count, 1, hidden), bf16),
            compiler_params=params(58),
            cost_estimate=matmul_cost(count * rows, feat_dim, hidden, 3 * count * MIB),
            name="code_grad",
        )(slope, emit_full, pre_slope, gh)

    add = lambda *terms: sum(t.astype(f32) for t in terms).astype(bf16)
    swap_core = lambda v: lax.ppermute(v, "client", xor_pairs(client_size, 1))
    top_bit = emits // 2
    got_a = swap_core(send_a)
    sum_a = add(keep_a, got_a)
    sum_a, code, gh = lax.optimization_barrier((sum_a, code, gh))
    from_pair = lax.ppermute(sum_a, "emit", xor_pairs(emits, top_bit))
    early = (slots * 3) // 4
    early_sum, keep_b, send_b = both_grads(early, gh, code)
    value = add(keep_b, swap_core(send_b), from_pair)
    value, gh = lax.optimization_barrier((value, gh))
    grad_pre = jnp.concatenate([early_sum, code_grad(early, slots - early, gh)])[:, 0]

    emit_bits, client_bits = bits_of(emits)[:-1][::-1], bits_of(client_size)[1:]
    value = value.reshape((2,) * (len(emit_bits) + len(client_bits)) + (block, feat_dim))
    for bit in emit_bits:
        value = halve(value, 0, "emit", emits, bit, emit_index)
    value = halve(value, value.ndim - 3, "client", client_size, client_bits[0], client_index)
    blocks = grad_pre.reshape(slots, emits * client_size, block).transpose(1, 0, 2)
    blocks, value = lax.optimization_barrier((blocks, value))
    value = value.reshape(client_size // 4, block, feat_dim)
    own = client_index // 4
    pieces = [lax.dynamic_index_in_dim(value, own, 0, keepdims=False)]
    for k in range(1, client_size // 4):
        send = lax.dynamic_index_in_dim(value, own ^ k, 0, keepdims=False)
        pieces.append(lax.ppermute(send, "client", xor_pairs(client_size, 4 * k)))
    value = sum(piece.astype(f32) for piece in pieces)
    emit_grad = value

    got = lax.all_to_all(blocks, ("emit", "client"), 0, 0)
    got = got.reshape(emits, clients, block).astype(f32)
    grad_slots = jnp.sum(got, axis=0).astype(bf16)
    grad_client = lax.dot_general(
        picker, grad_slots, (((0,), (0,)), ((), ())), preferred_element_type=f32
    ).astype(bf16)
    trunk_grad = lax.dot_general(
        trunk_in, grad_client, (((0,), (0,)), ((), ())), preferred_element_type=f32
    )
    return (loss, emit_grad, trunk_grad)


def solution(mesh):
    return jax.shard_map(
        per_device,
        mesh=mesh,
        in_specs=(
            P("client", None),
            P("client"),
            P(),
            P(),
            P(None, "client"),
            P("emit", None),
            P("emit", None),
        ),
        out_specs=(P("client"), P(("emit", "client"), None), P(None, ("emit", "client"))),
        check_vma=False,
    )
```

time: 302 us -> 168 us (0.56)
  Pallas kernels: 0 us -> 94.1 us
  matrix products: 96.5 us -> 3.3 us
  blocking collectives: 61.9 us -> 0 us
  waiting for transfers between devices: 68.1 us -> 30.9 us
  local copies, waits for them, and re-layouts: 37.1 us -> 4.21 us
  starting transfers between devices: 0.16 us -> 23 us
  between operations: 13.8 us -> 0.82 us
  other arithmetic: 23.4 us -> 10.8 us
    pallas_call x0 -> x5, Pallas kernels: none -> 94.1 us  [the longest x1 26.3 us: both_grads(): pl.pallas_call(functools.partial(both_grads_kernel, block, count, slots),...]
    dot_general x8 -> x2, matrix products: 96.5 us -> 3.3 us  [the longest x1 2.08 us: per_device(): jnp.dot(picker, pre_cols, preferred_element_type=f32).astype(bf16)]
    reduce_scatter x3 -> x0, waiting for transfers between devices: 67.3 us -> none  [the longest x1 39 us: per_device(): lax.psum_scatter(partial_rows, 'client', scatter_dimension=0, tiled=True)]
    all_gather x2 -> x0, blocking collectives: 46.6 us -> none  [the longest x1 24.6 us: per_device(): pre_all = lax.all_gather(pre_cols, 'client', axis=1, tiled=True)]
    add x1 -> x0, local copies, waits for them, and re-layouts: 29.4 us -> none  [per_device(): jax.nn.silu(pre_own)[:, None, :]]
    ppermute x0 -> x10, waiting for transfers between devices: none -> 25.4 us  [the longest x1 13.6 us: gather_emit(): lax.ppermute(mine, 'emit', xor_pairs(emits, bit))]
    all_to_all x0 -> x2, starting transfers between devices: none -> 12.1 us  [the longest x1 7.39 us: per_device(): lax.all_to_all(pre_slots.reshape(client_size, slots, hidden // client_siz...]
    add x2 -> x1, other arithmetic: 12.5 us -> 0.73 us  [per_device(): value = sum((piece.astype(f32) for piece in pieces))]
  transfers between devices with their start and end apart: 4 -> 12, of which waited for: 3 -> 8; matrix products, arithmetic and copies ran while one was open for 25% -> 5% of each run, Pallas kernels for 0% -> 29%
where the time goes in v1:
time: 168 us; the launch traced here: 167 us
  Pallas kernels  94.1 us (56%)
  waiting for transfers between devices  30.9 us (18%)
  starting transfers between devices  23 us (14%)
  other arithmetic  10.8 us (6%)
  local copies, waits for them, and re-layouts  4.21 us (3%)
  matrix products  3.3 us (2%)
    pallas_call x1, Pallas kernels, both_grads(): pl.pallas_call(functools.partial(both_grads_kernel, block, count, slots),...  26.3 us
    pallas_call x1, Pallas kernels, per_device(): pl.pallas_call(functools.partial(forward_kernel, classes), grid_spec=pltp...  24.8 us
    pallas_call x1, Pallas kernels, per_device(): pl.pallas_call(functools.partial(head_grad_kernel, 1.0 / clients, block,...  21.2 us
    pallas_call x1, Pallas kernels, per_device(): code, slope = make_code(act, class_table)  14.8 us
    ppermute x1, waiting for transfers between devices, gather_emit(): lax.ppermute(mine, 'emit', xor_pairs(emits, bit))  13.6 us
    all_to_all x1, starting transfers between devices, per_device(): lax.all_to_all(pre_slots.reshape(client_size, slots, hidden // client_siz...  7.39 us
    pallas_call x1, Pallas kernels, code_grad(): pl.pallas_call(code_grad_kernel, grid=(count,), in_specs=[pl.BlockSpec((r...  7.11 us
    all_to_all x1, starting transfers between devices, per_device(): got = lax.all_to_all(blocks, ('emit', 'client'), 0, 0)  4.7 us
  transfers between devices with their start and end apart: 12, of which 8 were waited for; matrix products, arithmetic and copies ran while one was open for 5% of the time, Pallas kernels for 29%

profile of v1, /device:TPU:0, one launch (start us, length us, event | category | flops | bytes accessed | tf_op | source)
XLA Modules:
  0.0 167.2 jit_solution(16594912995039088770)
XLA Ops:
  0.7 1.0 copy-done
  1.7 2.1 %convolution_convert_fusion = bf16[128,128]{1,0:T(8,128)(2,1)} fusion(bf16[128,2048]{1,0:T(8,128)(2,1)S(1)} %copy-done, bf16[2048,128]{1,0:T(8,128)(2,1)} %param.11, s32[128]{0:T(128)} %param.9), kind=kOutput, calls=%fused_computation.3 | convolution fusion | flops 71352320 | bytes 1081856 | tf_op jit(solution)/shard_map/dot_general | solution.py:202
  3.8 7.4 %all-to-all-start = ((bf16[16,8,128]{2,1,0:T(8,128)(2,1)}), bf16[16,8,128]{2,1,0:T(8,128)(2,1)S(1)}, u32[]{:S(2)}, u32[]{:S(2)}) async-start(bf16[16,8,128]{2,1,0:T(8,128)(2,1)} %bitcast.2), calls=%async_computation | async-start | bytes 65536 | tf_op jit(solution)/shard_map/all_to_all | solution.py:204
  11.2 1.2 dynamic-slice_bitcast_fusion
  12.4 1.6 collective-permute-start
  15.2 2.6 %all-to-all-done = bf16[16,8,128]{2,1,0:T(8,128)(2,1)S(1)} async-done(((bf16[16,8,128]{2,1,0:T(8,128)(2,1)}), bf16[16,8,128]{2,1,0:T(8,128)(2,1)S(1)}, u32[]{:S(2)}, u32[]{:S(2)}) %all-to-all-start) | async-done | bytes 32800 | tf_op jit(solution)/shard_map/all_to_all | solution.py:204
  17.8 0.8 add_multiply_fusion
  18.6 13.6 %collective-permute-done.mine_ref = bf16[1,512,768]{2,1,0:T(8,128)(2,1)S(1)} collective-permute-done((bf16[1,512,768]{2,1,0:T(8,128)(2,1)S(1)}, bf16[1,512,768]{2,1,0:T(8,128)(2,1)S(1)}, u32[]{:S(2)}, u32[]{:S(2)}) %collective-permute-start) | collective-permute-done | bytes 786464 | tf_op jit(solution)/shard_map/ppermute | solution.py:173
  32.3 0.8 multiply_multiply_fusion.act_ref
  33.1 14.8 %code.1 = (bf16[4096,2048]{1,0:T(8,128)(2,1)}, bf16[4096,2048]{1,0:T(8,128)(2,1)}) custom-call(f32[8,1,2048]{2,1,0:T(1,128)} %multiply_multiply_fusion.act_ref, bf16[500,2048]{1,0:T(8,128)(2,1)} %table_ref.1), custom_call_target="tpu_custom_call" | custom-call | flops 4000000000 | bytes 33554432 | tf_op jit(solution)/shard_map/code/pallas_call | solution.py:233
  47.9 0.9 copy-done.5
  48.8 24.8 %forward.1 = (f32[4096,512]{1,0:T(8,128)}, f32[8,3,512]{2,1,0:T(4,128)}, bf16[2048,768]{1,0:T(8,128)(2,1)}) custom-call(s32[3]{0:T(128)} %pad_add_fusion.where_ref, bf16[4096,2048]{1,0:T(8,128)(2,1)} %get-tuple-element.34.code_ref, bf16[1024,768]{1,0:T(8,128)(2,1)} %local_ref.1, bf16[1,512,768]{2,1,0:T(8,128)(2,1)} %copy-done.4, ...), custom_call_target="tpu_custom_call" | custom-call | flops 16106127360 | bytes 31457280 | tf_op jit(solution)/shard_map/forward/pallas_call | solution.py:235
  73.6 1.6 collective-permute-start.2
  75.7 2.5 %collective-permute-done.2 = f32[8,3,512]{2,1,0:T(4,128)S(1)} collective-permute-done((f32[8,3,512]{2,1,0:T(4,128)}, f32[8,3,512]{2,1,0:T(4,128)S(1)}, u32[]{:S(2)}, u32[]{:S(2)}) %collective-permute-start.2) | collective-permute-done | bytes 49184 | tf_op jit(solution)/shard_map/ppermute | solution.py:267
  78.2 1.7 add_divide_fusion.1
  79.9 21.2 %head_grad.1 = (bf16[4096,768]{1,0:T(8,128)(2,1)}, bf16[512,768]{1,0:T(8,128)(2,1)}, bf16[512,768]{1,0:T(8,128)(2,1)}) custom-call(s32[2]{0:T(128)} %pad_add_fusion.2.where_ref, f32[4096,512]{1,0:T(8,128)} %get-tuple-element.29.p_ref, f32[8,1,512]{2,1,0:T(1,128)} %get-tuple-element.48.scale_ref, s32[8,1,512]{2,1,0:T(1,128)} %bitcast.56, ...), custom_call_target="tpu_custom_call" | custom-call | flops 9663676416 | bytes 20971520 | tf_op jit(solution)/shard_map/head_grad/pallas_call | solution.py:283
  101.7 1.9 %collective-permute-done.3 = bf16[512,768]{1,0:T(8,128)(2,1)S(1)} collective-permute-done((bf16[512,768]{1,0:T(8,128)(2,1)}, bf16[512,768]{1,0:T(8,128)(2,1)S(1)}, u32[]{:S(2)}, u32[]{:S(2)}) %collective-permute-start.3) | collective-permute-done | bytes 786464 | tf_op jit(solution)/shard_map/ppermute | solution.py:349
  103.6 1.3 add_convert_fusion.1
  104.9 1.6 collective-permute-start.5
  106.5 26.3 %both_grads.1 = (bf16[6,1,2048]{2,1,0:T(2,128)(2,1)}, bf16[512,768]{1,0:T(8,128)(2,1)}, bf16[512,768]{1,0:T(8,128)(2,1)}) custom-call(s32[2]{0:T(128)} %pad_add_fusion.1.where_ref, bf16[4096,2048]{1,0:T(8,128)(2,1)} %get-tuple-element.27.slope_ref, bf16[2048,768]{1,0:T(8,128)(2,1)} %get-tuple-element.28.emit_ref, ...), custom_call_target="tpu_custom_call" | custom-call | flops 16106127360 | bytes 31457280 | tf_op jit(solution)/shard_map/both_grads/pallas_call | solution.py:307
  132.8 2.4 %collective-permute-done.4 = bf16[512,768]{1,0:T(8,128)(2,1)S(1)} collective-permute-done((bf16[512,768]{1,0:T(8,128)(2,1)}, bf16[512,768]{1,0:T(8,128)(2,1)S(1)}, u32[]{:S(2)}, u32[]{:S(2)}) %collective-permute-start.4) | collective-permute-done | bytes 786464 | tf_op jit(solution)/shard_map/ppermute | solution.py:349
  135.3 1.4 add_convert_fusion
  136.7 1.7 %collective-permute-start.6 = (bf16[2,2,64,768]{3,2,1,0:T(8,128)(2,1)S(1)}, bf16[2,2,64,768]{3,2,1,0:T(8,128)(2,1)S(1)}, u32[]{:S(2)}, u32[]{:S(2)}) collective-permute-start(bf16[2,2,64,768]{3,2,1,0:T(8,128)(2,1)S(1)} %dynamic-slice_bitcast_fusion.1), channel_id=1, source_target_pairs={{0,2},{1,3},{2,0},{3,1},{4,6},{5,7},{6,4},{7,5},{8,10},{9,11},{10,... | collective-permute-start | bytes 1179656 | tf_op jit(solution)/shard_map/ppermute | solution.py:182
  139.1 7.1 %code_grad.1 = bf16[2,1,2048]{2,1,0:T(2,128)(2,1)} custom-call(bf16[4096,2048]{1,0:T(8,128)(2,1)} %get-tuple-element.27.slope_ref, bf16[2048,768]{1,0:T(8,128)(2,1)} %get-tuple-element.28.emit_ref, f32[8,1,2048]{2,1,0:T(1,128)} %get-tuple-element.43.pre_slope_ref, bf16[4096,768]{1,0:T(8,128)(2,1)} %get-tuple-element.39.gh_ref), custom_call_target="tpu_custom_call" | custom-call | flops 3221225472 | bytes 6291456 | tf_op jit(solution)/shard_map/code_grad/pallas_call | solution.py:332
  146.2 0.9 maximum_reduce_fusion
  147.2 0.8 collective-permute-done.6
  148.8 4.7 %all-to-all-start.1 = ((bf16[32,2,256]{2,1,0:T(2,128)(2,1)}), bf16[32,2,256]{2,1,0:T(2,128)(2,1)S(1)}, u32[]{:S(2)}, u32[]{:S(2)}) async-start(bf16[32,2,256]{2,1,0:T(2,128)(2,1)} %reshape.90), calls=%async_computation.1 | async-start | bytes 65536 | tf_op jit(solution)/shard_map/all_to_all | solution.py:377
  153.6 3.7 %collective-permute-start.9 = (bf16[64,768]{1,0:T(8,128)(2,1)S(1)}, bf16[64,768]{1,0:T(8,128)(2,1)S(1)}, u32[]{:S(2)}, u32[]{:S(2)}) collective-permute-start(bf16[64,768]{1,0:T(8,128)(2,1)S(1)} %get-tuple-element.46), channel_id=1, source_target_pairs={{0,12},{1,13},{2,14},{3,15},{4,8},{5,9},{6,10},{7,11},{8,4},{9,5},... | collective-permute-start | bytes 294920 | tf_op jit(solution)/shard_map/ppermute | solution.py:373
  157.3 0.8 collective-permute-start.7
  158.0 2.9 %all-to-all-done.1 = bf16[32,2,256]{2,1,0:T(2,128)(2,1)S(1)} async-done(((bf16[32,2,256]{2,1,0:T(2,128)(2,1)}), bf16[32,2,256]{2,1,0:T(2,128)(2,1)S(1)}, u32[]{:S(2)}, u32[]{:S(2)}) %all-to-all-start.1) | async-done | bytes 32800 | tf_op jit(solution)/shard_map/all_to_all | solution.py:377
  161.1 1.2 convolution_bitcast_fusion
  162.3 4.2 %collective-permute-done.8 = bf16[64,768]{1,0:T(8,128)(2,1)S(1)} collective-permute-done((bf16[64,768]{1,0:T(8,128)(2,1)S(1)}, bf16[64,768]{1,0:T(8,128)(2,1)S(1)}, u32[]{:S(2)}, u32[]{:S(2)}) %collective-permute-start.8) | collective-permute-done | bytes 98336 | tf_op jit(solution)/shard_map/ppermute | solution.py:373
  (34 shorter events, 5.0 us)
Async XLA Ops:
  0.6 1.0 copy-start
  0.6 13.3 %copy-start.2 = (s32[4096]{0:T(1024)S(1)}, s32[4096]{0:T(1024)}, u32[]{:S(2)}) copy-start(s32[4096]{0:T(1024)} %param.8) | copy-start | bytes 49156
  3.8 14.0 %all-to-all-start = ((bf16[16,8,128]{2,1,0:T(8,128)(2,1)}), bf16[16,8,128]{2,1,0:T(8,128)(2,1)S(1)}, u32[]{:S(2)}, u32[]{:S(2)}) async-start(bf16[16,8,128]{2,1,0:T(8,128)(2,1)} %bitcast.2), calls=%async_computation | async-start | bytes 65536 | tf_op jit(solution)/shard_map/all_to_all | solution.py:204
  12.4 19.9 %collective-permute-start = (bf16[1,512,768]{2,1,0:T(8,128)(2,1)S(1)}, bf16[1,512,768]{2,1,0:T(8,128)(2,1)S(1)}, u32[]{:S(2)}, u32[]{:S(2)}) collective-permute-start(bf16[1,512,768]{2,1,0:T(8,128)(2,1)S(1)} %dynamic-slice_bitcast_fusion), channel_id=1, source_target_pairs={{0,16},{16,0},{1,17},{17,1},{2,18},{18,2},{3,19},{19,3},{4,20},{20... | collective-permute-start | bytes 2359304 | tf_op jit(solution)/shard_map/ppermute | solution.py:173
  32.3 15.6 %copy-start.4 = (bf16[1,512,768]{2,1,0:T(8,128)(2,1)}, bf16[1,512,768]{2,1,0:T(8,128)(2,1)S(1)}, u32[]{:S(2)}) copy-start(bf16[1,512,768]{2,1,0:T(8,128)(2,1)S(1)} %collective-permute-done.mine_ref) | copy-start | bytes 2359300
  32.3 15.6 %collective-permute-start.1 = (bf16[1,512,768]{2,1,0:T(8,128)(2,1)S(1)}, bf16[1,512,768]{2,1,0:T(8,128)(2,1)S(1)}, u32[]{:S(2)}, u32[]{:S(2)}) collective-permute-start(bf16[1,512,768]{2,1,0:T(8,128)(2,1)S(1)} %collective-permute-done.mine_ref), channel_id=1, source_target_pairs={{0,1},{1,0},{2,3},{3,2},{4,5},{5,4},{6,7},{7,6},{8,9},{9,8},{10,11... | collective-permute-start | bytes 2359304 | tf_op jit(solution)/shard_map/ppermute | solution.py:174
  47.9 0.9 copy-start.5
  73.6 4.7 %collective-permute-start.2 = (f32[8,3,512]{2,1,0:T(4,128)}, f32[8,3,512]{2,1,0:T(4,128)S(1)}, u32[]{:S(2)}, u32[]{:S(2)}) collective-permute-start(f32[8,3,512]{2,1,0:T(4,128)} %get-tuple-element.26), channel_id=1, source_target_pairs={{0,16},{16,0},{1,17},{17,1},{2,18},{18,2},{3,19},{19,3},{4,20},{20... | collective-permute-start | bytes 147464 | tf_op jit(solution)/shard_map/ppermute | solution.py:267
  101.1 2.5 %collective-permute-start.3 = (bf16[512,768]{1,0:T(8,128)(2,1)}, bf16[512,768]{1,0:T(8,128)(2,1)S(1)}, u32[]{:S(2)}, u32[]{:S(2)}) collective-permute-start(bf16[512,768]{1,0:T(8,128)(2,1)} %get-tuple-element.31), channel_id=1, source_target_pairs={{0,1},{1,0},{2,3},{3,2},{4,5},{5,4},{6,7},{7,6},{8,9},{9,8},{10,11... | collective-permute-start | bytes 2359304 | tf_op jit(solution)/shard_map/ppermute | solution.py:349
  104.9 28.0 %collective-permute-start.5 = (bf16[512,768]{1,0:T(8,128)(2,1)S(1)}, bf16[512,768]{1,0:T(8,128)(2,1)S(1)}, u32[]{:S(2)}, u32[]{:S(2)}) collective-permute-start(bf16[512,768]{1,0:T(8,128)(2,1)S(1)} %add_convert_fusion.1), channel_id=1, source_target_pairs={{0,16},{16,0},{1,17},{17,1},{2,18},{18,2},{3,19},{19,3},{4,20},{20... | collective-permute-start | bytes 2359304 | tf_op jit(solution)/shard_map/ppermute | solution.py:354
  132.8 2.5 %collective-permute-start.4 = (bf16[512,768]{1,0:T(8,128)(2,1)}, bf16[512,768]{1,0:T(8,128)(2,1)S(1)}, u32[]{:S(2)}, u32[]{:S(2)}) collective-permute-start(bf16[512,768]{1,0:T(8,128)(2,1)} %get-tuple-element.37), channel_id=1, source_target_pairs={{0,1},{1,0},{2,3},{3,2},{4,5},{5,4},{6,7},{7,6},{8,9},{9,8},{10,11... | collective-permute-start | bytes 2359304 | tf_op jit(solution)/shard_map/ppermute | solution.py:349
  136.7 11.2 %collective-permute-start.6 = (bf16[2,2,64,768]{3,2,1,0:T(8,128)(2,1)S(1)}, bf16[2,2,64,768]{3,2,1,0:T(8,128)(2,1)S(1)}, u32[]{:S(2)}, u32[]{:S(2)}) collective-permute-start(bf16[2,2,64,768]{3,2,1,0:T(8,128)(2,1)S(1)} %dynamic-slice_bitcast_fusion.1), channel_id=1, source_target_pairs={{0,2},{1,3},{2,0},{3,1},{4,6},{5,7},{6,4},{7,5},{8,10},{9,11},{10,... | collective-permute-start | bytes 1179656 | tf_op jit(solution)/shard_map/ppermute | solution.py:182
  139.1 7.1 %copy-start.1 = (bf16[6,1,2048]{2,1,0:T(2,128)(2,1)S(1)}, bf16[6,1,2048]{2,1,0:T(2,128)(2,1)}, u32[]{:S(2)}) copy-start(bf16[6,1,2048]{2,1,0:T(2,128)(2,1)} %get-tuple-element.35) | copy-start | bytes 73732
  146.2 14.9 %copy-start.3 = (s32[128]{0:T(128)S(1)}, s32[128]{0:T(128)}, u32[]{:S(2)}) copy-start(s32[128]{0:T(128)} %param.9) | copy-start | bytes 1540
  148.8 12.1 %all-to-all-start.1 = ((bf16[32,2,256]{2,1,0:T(2,128)(2,1)}), bf16[32,2,256]{2,1,0:T(2,128)(2,1)S(1)}, u32[]{:S(2)}, u32[]{:S(2)}) async-start(bf16[32,2,256]{2,1,0:T(2,128)(2,1)} %reshape.90), calls=%async_computation.1 | async-start | bytes 65536 | tf_op jit(solution)/shard_map/all_to_all | solution.py:377
  153.6 8.7 %collective-permute-start.9 = (bf16[64,768]{1,0:T(8,128)(2,1)S(1)}, bf16[64,768]{1,0:T(8,128)(2,1)S(1)}, u32[]{:S(2)}, u32[]{:S(2)}) collective-permute-start(bf16[64,768]{1,0:T(8,128)(2,1)S(1)} %get-tuple-element.46), channel_id=1, source_target_pairs={{0,12},{1,13},{2,14},{3,15},{4,8},{5,9},{6,10},{7,11},{8,4},{9,5},... | collective-permute-start | bytes 294920 | tf_op jit(solution)/shard_map/ppermute | solution.py:373
  157.3 9.2 %collective-permute-start.8 = (bf16[64,768]{1,0:T(8,128)(2,1)S(1)}, bf16[64,768]{1,0:T(8,128)(2,1)S(1)}, u32[]{:S(2)}, u32[]{:S(2)}) collective-permute-start(bf16[64,768]{1,0:T(8,128)(2,1)S(1)} %get-tuple-element.47), channel_id=1, source_target_pairs={{0,8},{1,9},{2,10},{3,11},{4,12},{5,13},{6,14},{7,15},{8,0},{9,1},... | collective-permute-start | bytes 294920 | tf_op jit(solution)/shard_map/ppermute | solution.py:373
  157.3 9.2 %collective-permute-start.7 = (bf16[64,768]{1,0:T(8,128)(2,1)S(1)}, bf16[64,768]{1,0:T(8,128)(2,1)S(1)}, u32[]{:S(2)}, u32[]{:S(2)}) collective-permute-start(bf16[64,768]{1,0:T(8,128)(2,1)S(1)} %get-tuple-element.45), channel_id=1, source_target_pairs={{0,4},{1,5},{2,6},{3,7},{4,0},{5,1},{6,2},{7,3},{8,12},{9,13},{10,... | collective-permute-start | bytes 294920 | tf_op jit(solution)/shard_map/ppermute | solution.py:373

commit v2 on v1

--- a/solution.py
+++ b/solution.py
@@ -72,7 +72,7 @@
         logits = jnp.where(number < classes, logits, -jnp.inf)
         top = jnp.max(logits, axis=0, keepdims=True)
         p = jnp.exp(logits - top)
-        p_ref[...] = p
+        p_ref[...] = p.astype(jnp.bfloat16)
         stat_ref[0, 0:1, :] = top
         stat_ref[0, 1:2, :] = jnp.sum(p, axis=0, keepdims=True)
         stat_ref[0, 2:3, :] = target
@@ -102,15 +102,15 @@
     send_ref[...] = jnp.where(is_first, second, first).astype(jnp.bfloat16)
 
 
-def head_grad_kernel(inv_clients, block, slots, where_ref, p_ref, scale_ref, label_ref, feat_ref, code_ref, gh_ref, keep_ref, send_ref, all_ref):
+def head_grad_kernel(block, slots, where_ref, p_ref, scale_ref, at_label_ref, label_ref, feat_ref, code_ref, gh_ref, keep_ref, send_ref, all_ref):
     step = pl.program_id(0)
     rows = p_ref.shape[0]
 
     @pl.when(step < slots)
     def _():
         number = lax.broadcasted_iota(jnp.int32, p_ref.shape, 0)
-        soft = p_ref[...] * scale_ref[0]
-        grad = (soft - jnp.where(number == label_ref[0], 1.0, 0.0)) * inv_clients
+        grad = p_ref[...].astype(jnp.float32) * scale_ref[0]
+        grad = jnp.where(number == label_ref[0], at_label_ref[0], grad)
         gh = jnp.dot(
             grad.astype(jnp.bfloat16), feat_ref[...], preferred_element_type=jnp.float32
         ).astype(jnp.bfloat16)
@@ -139,21 +139,8 @@
     store_code_grad(gh_ref[...], slope_ref, emit_ref, pre_slope_ref, out_ref)
 
 
-def both_grads_kernel(block, count, slots, where_ref, slope_ref, emit_ref, pre_slope_ref, gh_ref, code_ref, out_ref, keep_ref, send_ref, all_ref):
-    step = pl.program_id(0)
-    rows = slope_ref.shape[0]
-
-    @pl.when(step < count)
-    def _():
-        store_code_grad(gh_ref[...], slope_ref, emit_ref, pre_slope_ref, out_ref)
-
-    @pl.when(step < slots)
-    def _():
-        all_ref[pl.ds(pl.multiple_of(step * rows, rows), rows), :] = gh_ref[...]
-
-    @pl.when(step >= slots)
-    def _():
-        store_emit_grad(block, where_ref[1] == 0, code_ref[...], all_ref[...], keep_ref, send_ref)
+def emit_grad_kernel(block, where_ref, gh_ref, code_ref, keep_ref, send_ref):
+    store_emit_grad(block, where_ref[1] == 0, code_ref[...], gh_ref[...], keep_ref, send_ref)
 
 
 def xor_pairs(size, bit):
@@ -253,7 +240,7 @@
             scratch_shapes=[pltpu.VMEM((rows, feat_dim), bf16)],
         ),
         out_shape=[
-            jax.ShapeDtypeStruct((slots * rows, samples), f32),
+            jax.ShapeDtypeStruct((slots * rows, samples), bf16),
             pltpu.HBM((slots, 3, samples), f32),
             pltpu.HBM((hidden, feat_dim), bf16),
         ],
@@ -270,7 +257,8 @@
         target = target + other[:, 2]
         top = new_top
     loss = (top + jnp.log(total) - target).reshape(slots * samples)
-    scale = (jnp.exp(stats[:, 0] - top) / total)[:, None, :]
+    scale = (jnp.exp(stats[:, 0] - top) / (total * clients))[:, None, :]
+    at_label = ((jnp.exp(target - top) / total - 1.0) / clients)[:, None, :]
 
     block = hidden // (emits * client_size)
     width = min(256, hidden // 2)
@@ -281,12 +269,13 @@
     step_of = lambda s: jnp.maximum(s - slots, 0)
 
     gh, keep_a, send_a = pl.pallas_call(
-        functools.partial(head_grad_kernel, 1.0 / clients, block, slots),
+        functools.partial(head_grad_kernel, block, slots),
         grid_spec=pltpu.PrefetchScalarGridSpec(
             num_scalar_prefetch=1,
             grid=(slots + steps,),
             in_specs=[
                 pl.BlockSpec((rows, samples), lambda s, w: (slot_of(s), 0)),
+                pl.BlockSpec((1, 1, samples), lambda s, w: (slot_of(s), 0, 0)),
                 pl.BlockSpec((1, 1, samples), lambda s, w: (slot_of(s), 0, 0)),
                 pl.BlockSpec((1, 1, samples), lambda s, w: (slot_of(s), 0, 0)),
                 pl.BlockSpec((samples, feat_dim), lambda s, w: (slot_of(s), 0)),
@@ -300,33 +289,25 @@
         compiler_params=params(58),
         cost_estimate=matmul_cost(feat_dim, slots * rows, hidden // 2 + samples, 20 * MIB),
         name="head_grad",
-    )(at(1 - where[2]), p, scale, local, features, code)
-
-    def both_grads(count, gh, code):
-        early_of = lambda s: jnp.minimum(s, count - 1)
+    )(at(1 - where[2]), p, scale, at_label, local, features, code)
+
+    def emit_rest(gh, code):
         return pl.pallas_call(
-            functools.partial(both_grads_kernel, block, count, slots),
+            functools.partial(emit_grad_kernel, block),
             grid_spec=pltpu.PrefetchScalarGridSpec(
                 num_scalar_prefetch=1,
-                grid=(slots + steps,),
+                grid=(steps,),
                 in_specs=[
-                    pl.BlockSpec((rows, hidden), lambda s, w: (early_of(s), 0)),
-                    whole((hidden, feat_dim)),
-                    pl.BlockSpec((1, 1, hidden), lambda s, w: (early_of(s), 0, 0)),
-                    pl.BlockSpec((rows, feat_dim), lambda s, w: (slot_of(s), 0)),
-                    pl.BlockSpec((slots * rows, width), lambda s, w: (0, w[0] + step_of(s))),
+                    whole((slots * rows, feat_dim)),
+                    pl.BlockSpec((slots * rows, width), lambda h, w: (0, w[0] + h)),
                 ],
-                out_specs=[pl.BlockSpec((1, 1, hidden), lambda s, w: (early_of(s), 0, 0))]
-                + [pl.BlockSpec((width // 2, feat_dim), lambda s, w: (step_of(s), 0))] * 2,
-                scratch_shapes=[pltpu.VMEM((slots * rows, feat_dim), bf16)],
+                out_specs=[pl.BlockSpec((width // 2, feat_dim), lambda h, w: (h, 0))] * 2,
             ),
-            out_shape=[jax.ShapeDtypeStruct((count, 1, hidden), bf16)] + halves,
+            out_shape=halves,
             compiler_params=params(58),
-            cost_estimate=matmul_cost(
-                feat_dim, slots * rows, hidden // 2 + hidden * count // slots, 30 * MIB
-            ),
-            name="both_grads",
-        )(at(where[2]), slope, emit_full, pre_slope, gh, code)
+            cost_estimate=matmul_cost(feat_dim, slots * rows, hidden // 2, 12 * MIB),
+            name="emit_grad",
+        )(at(where[2]), gh, code)
 
     def code_grad(first, count, gh):
         return pl.pallas_call(
@@ -352,9 +333,12 @@
     sum_a = add(keep_a, got_a)
     sum_a, code, gh = lax.optimization_barrier((sum_a, code, gh))
     from_pair = lax.ppermute(sum_a, "emit", xor_pairs(emits, top_bit))
-    early = (slots * 3) // 4
-    early_sum, keep_b, send_b = both_grads(early, gh, code)
-    value = add(keep_b, swap_core(send_b), from_pair)
+    keep_b, send_b = emit_rest(gh, code)
+    send_b, gh = lax.optimization_barrier((send_b, gh))
+    got_b = swap_core(send_b)
+    early = slots // 2
+    early_sum = code_grad(0, early, gh)
+    value = add(keep_b, got_b, from_pair)
     value, gh = lax.optimization_barrier((value, gh))
     grad_pre = jnp.concatenate([early_sum, code_grad(early, slots - early, gh)])[:, 0]
 

time: 168 us -> 163 us (0.970)
  waiting for transfers between devices: 30.9 us -> 27.7 us
    pallas_call x2, Pallas kernels: 47.5 us -> 31.9 us  [the longest x1 19.6 us: per_device(): pl.pallas_call(functools.partial(head_grad_kernel, block, slots), grid_sp...]
    pallas_call x1 -> x2, Pallas kernels: 7.11 us -> 21.8 us  [code_grad(): pl.pallas_call(code_grad_kernel, grid=(count,), in_specs=[pl.BlockSpec((r...]
    ppermute x2, waiting for transfers between devices: 4.34 us -> 1.86 us  [per_device(): swap_core = lambda v: lax.ppermute(v, 'client', xor_pairs(client_size, 1))]
  transfers between devices with their start and end apart: 12 -> 12, of which waited for: 8 -> 6; matrix products, arithmetic and copies ran while one was open for 5% -> 5% of each run, Pallas kernels for 29% -> 30%
where the time goes in v2:
time: 163 us
  Pallas kernels  93.4 us (57%)
  waiting for transfers between devices  27.7 us (17%)
  starting transfers between devices  21.9 us (13%)
  other arithmetic  11.4 us (7%)
  local copies, waits for them, and re-layouts  4.2 us (3%)
  matrix products  3.3 us (2%)
    pallas_call x1, Pallas kernels, per_device(): pl.pallas_call(functools.partial(forward_kernel, classes), grid_spec=pltp...  24.9 us
    pallas_call x2, Pallas kernels, code_grad(): pl.pallas_call(code_grad_kernel, grid=(count,), in_specs=[pl.BlockSpec((r...  21.8 us
    pallas_call x1, Pallas kernels, per_device(): pl.pallas_call(functools.partial(head_grad_kernel, block, slots), grid_sp...  19.6 us
    pallas_call x1, Pallas kernels, per_device(): code, slope = make_code(act, class_table)  14.8 us
    ppermute x1, waiting for transfers between devices, gather_emit(): lax.ppermute(mine, 'emit', xor_pairs(emits, bit))  13.6 us
    pallas_call x1, Pallas kernels, emit_rest(): pl.pallas_call(functools.partial(emit_grad_kernel, block), grid_spec=pltp...  12.3 us
    all_to_all x1, starting transfers between devices, per_device(): lax.all_to_all(pre_slots.reshape(client_size, slots, hidden // client_siz...  7.39 us
    ppermute x3, starting transfers between devices, per_device(): pieces.append(lax.ppermute(send, 'client', xor_pairs(client_size, 4 * k)))  4.45 us
  transfers between devices with their start and end apart: 12, of which 6 were waited for; matrix products, arithmetic and copies ran while one was open for 5% of the time, Pallas kernels for 30%

profile of v2, /device:TPU:0, one launch (start us, length us, event | category | flops | bytes accessed | tf_op | source)
XLA Modules:
  0.0 162.7 jit_solution(15161196336186179710)
XLA Ops:
  0.7 1.0 copy-done
  1.7 2.1 %convolution_convert_fusion = bf16[128,128]{1,0:T(8,128)(2,1)} fusion(bf16[128,2048]{1,0:T(8,128)(2,1)S(1)} %copy-done, bf16[2048,128]{1,0:T(8,128)(2,1)} %param.11, s32[128]{0:T(128)} %param.9), kind=kOutput, calls=%fused_computation.3 | convolution fusion | flops 71352320 | bytes 1081856 | tf_op jit(solution)/shard_map/dot_general | solution.py:189
  3.8 7.4 %all-to-all-start = ((bf16[16,8,128]{2,1,0:T(8,128)(2,1)}), bf16[16,8,128]{2,1,0:T(8,128)(2,1)S(1)}, u32[]{:S(2)}, u32[]{:S(2)}) async-start(bf16[16,8,128]{2,1,0:T(8,128)(2,1)} %bitcast.2), calls=%async_computation | async-start | bytes 65536 | tf_op jit(solution)/shard_map/all_to_all | solution.py:191
  11.2 1.2 dynamic-slice_bitcast_fusion
  12.4 1.6 collective-permute-start
  15.2 2.6 %all-to-all-done = bf16[16,8,128]{2,1,0:T(8,128)(2,1)S(1)} async-done(((bf16[16,8,128]{2,1,0:T(8,128)(2,1)}), bf16[16,8,128]{2,1,0:T(8,128)(2,1)S(1)}, u32[]{:S(2)}, u32[]{:S(2)}) %all-to-all-start) | async-done | bytes 32800 | tf_op jit(solution)/shard_map/all_to_all | solution.py:191
  17.8 0.8 add_multiply_fusion
  18.6 13.6 %collective-permute-done.mine_ref = bf16[1,512,768]{2,1,0:T(8,128)(2,1)S(1)} collective-permute-done((bf16[1,512,768]{2,1,0:T(8,128)(2,1)S(1)}, bf16[1,512,768]{2,1,0:T(8,128)(2,1)S(1)}, u32[]{:S(2)}, u32[]{:S(2)}) %collective-permute-start) | collective-permute-done | bytes 786464 | tf_op jit(solution)/shard_map/ppermute | solution.py:160
  32.3 0.8 multiply_multiply_fusion.act_ref
  33.1 14.8 %code.1 = (bf16[4096,2048]{1,0:T(8,128)(2,1)}, bf16[4096,2048]{1,0:T(8,128)(2,1)}) custom-call(f32[8,1,2048]{2,1,0:T(1,128)} %multiply_multiply_fusion.act_ref, bf16[500,2048]{1,0:T(8,128)(2,1)} %table_ref.1), custom_call_target="tpu_custom_call" | custom-call | flops 4000000000 | bytes 33554432 | tf_op jit(solution)/shard_map/code/pallas_call | solution.py:220
  47.9 0.9 copy-done.6
  48.8 24.9 %forward.1 = (bf16[4096,512]{1,0:T(8,128)(2,1)}, f32[8,3,512]{2,1,0:T(4,128)}, bf16[2048,768]{1,0:T(8,128)(2,1)}) custom-call(s32[3]{0:T(128)} %pad_add_fusion.where_ref, bf16[4096,2048]{1,0:T(8,128)(2,1)} %get-tuple-element.35.code_ref, bf16[1024,768]{1,0:T(8,128)(2,1)} %local_ref.1, bf16[1,512,768]{2,1,0:T(8,128)(2,1)} %copy-done.5, ...), custom_call_target="tpu_custom_call" | custom-call | flops 16106127360 | bytes 31457280 | tf_op jit(solution)/shard_map/forward/pallas_call | solution.py:222
  73.6 1.6 collective-permute-start.2
  75.8 2.5 %collective-permute-done.2 = f32[8,3,512]{2,1,0:T(4,128)S(1)} collective-permute-done((f32[8,3,512]{2,1,0:T(4,128)}, f32[8,3,512]{2,1,0:T(4,128)S(1)}, u32[]{:S(2)}, u32[]{:S(2)}) %collective-permute-start.2) | collective-permute-done | bytes 49184 | tf_op jit(solution)/shard_map/ppermute | solution.py:254
  78.3 1.7 %add_multiply_fusion.1 = (f32[8,1,512]{2,1,0:T(1,128)}, f32[8,1,512]{2,1,0:T(1,128)S(1)}, f32[8,1,512]{2,1,0:T(1,128)S(1)}) fusion(f32[8,3,512]{2,1,0:T(4,128)S(1)} %collective-permute-done.2, f32[8,3,512]{2,1,0:T(4,128)} %get-tuple-element.27), kind=kLoop, calls=%fused_computation.26 | loop fusion | flops 45056 | bytes 147456 | tf_op jit(solution)/shard_map/div | solution.py:261
  80.0 1.6 multiply_divide_fusion
  81.6 19.6 %head_grad.1 = (bf16[4096,768]{1,0:T(8,128)(2,1)}, bf16[512,768]{1,0:T(8,128)(2,1)}, bf16[512,768]{1,0:T(8,128)(2,1)}) custom-call(s32[2]{0:T(128)} %pad_add_fusion.2.where_ref, bf16[4096,512]{1,0:T(8,128)(2,1)} %get-tuple-element.30.p_ref, f32[8,1,512]{2,1,0:T(1,128)} %get-tuple-element.53.scale_ref, f32[8,1,512]{2,1,0:T(1,128)} %get-tuple-element.45.at_label_ref, ...), custom_call_target="tpu_custom_call" | custom-call | flops 9663676416 | bytes 20971520 | tf_op jit(solution)/shard_map/head_grad/pallas_call | solution.py:271
  101.9 1.9 %collective-permute-done.3 = bf16[512,768]{1,0:T(8,128)(2,1)S(1)} collective-permute-done((bf16[512,768]{1,0:T(8,128)(2,1)}, bf16[512,768]{1,0:T(8,128)(2,1)S(1)}, u32[]{:S(2)}, u32[]{:S(2)}) %collective-permute-start.3) | collective-permute-done | bytes 786464 | tf_op jit(solution)/shard_map/ppermute | solution.py:330
  103.7 1.3 add_convert_fusion.1
  105.0 1.6 collective-permute-start.5
  106.6 12.3 %emit_grad.1 = (bf16[512,768]{1,0:T(8,128)(2,1)}, bf16[512,768]{1,0:T(8,128)(2,1)}) custom-call(s32[2]{0:T(128)} %pad_add_fusion.1.where_ref, bf16[4096,768]{1,0:T(8,128)(2,1)} %get-tuple-element.41.gh_ref, bf16[4096,2048]{1,0:T(8,128)(2,1)} %get-tuple-element.35.code_ref), custom_call_target="tpu_custom_call" | custom-call | flops 6442450944 | bytes 12582912 | tf_op jit(solution)/shard_map/emit_grad/pallas_call | solution.py:295
  119.6 10.9 %code_grad.2 = bf16[4,1,2048]{2,1,0:T(2,128)(2,1)} custom-call(bf16[4096,2048]{1,0:T(8,128)(2,1)} %get-tuple-element.28.slope_ref, bf16[2048,768]{1,0:T(8,128)(2,1)} %get-tuple-element.29.emit_ref, f32[8,1,2048]{2,1,0:T(1,128)} %get-tuple-element.48.pre_slope_ref, bf16[4096,768]{1,0:T(8,128)(2,1)} %get-tuple-element.41.gh_ref), custom_call_target="tpu_custom_call" | custom-call | flops 6442450944 | bytes 12582912 | tf_op jit(solution)/shard_map/code_grad/pallas_call | solution.py:313
  130.8 1.7 %collective-permute-start.6 = (bf16[2,2,64,768]{3,2,1,0:T(8,128)(2,1)S(1)}, bf16[2,2,64,768]{3,2,1,0:T(8,128)(2,1)S(1)}, u32[]{:S(2)}, u32[]{:S(2)}) collective-permute-start(bf16[2,2,64,768]{3,2,1,0:T(8,128)(2,1)S(1)} %dynamic-slice_bitcast_fusion.1), channel_id=1, source_target_pairs={{0,2},{1,3},{2,0},{3,1},{4,6},{5,7},{6,4},{7,5},{8,10},{9,11},{10,... | collective-permute-start | bytes 1179656 | tf_op jit(solution)/shard_map/ppermute | solution.py:169
  132.5 10.9 %code_grad.3 = bf16[4,1,2048]{2,1,0:T(2,128)(2,1)} custom-call(bf16[4096,2048]{1,0:T(8,128)(2,1)} %get-tuple-element.28.slope_ref, bf16[2048,768]{1,0:T(8,128)(2,1)} %get-tuple-element.29.emit_ref, f32[8,1,2048]{2,1,0:T(1,128)} %get-tuple-element.48.pre_slope_ref, bf16[4096,768]{1,0:T(8,128)(2,1)} %get-tuple-element.41.gh_ref), custom_call_target="tpu_custom_call" | custom-call | flops 6442450944 | bytes 12582912 | tf_op jit(solution)/shard_map/code_grad/pallas_call | solution.py:313
  143.4 0.9 maximum_reduce_fusion
  144.6 0.7 reshape.90
  145.3 3.6 %all-to-all-start.1 = ((bf16[32,2,256]{2,1,0:T(2,128)(2,1)}), bf16[32,2,256]{2,1,0:T(2,128)(2,1)S(1)}, u32[]{:S(2)}, u32[]{:S(2)}) async-start(bf16[32,2,256]{2,1,0:T(2,128)(2,1)} %reshape.90), calls=%async_computation.1 | async-start | bytes 65536 | tf_op jit(solution)/shard_map/all_to_all | solution.py:361
  149.0 3.7 %collective-permute-start.9 = (bf16[64,768]{1,0:T(8,128)(2,1)S(1)}, bf16[64,768]{1,0:T(8,128)(2,1)S(1)}, u32[]{:S(2)}, u32[]{:S(2)}) collective-permute-start(bf16[64,768]{1,0:T(8,128)(2,1)S(1)} %get-tuple-element.51), channel_id=1, source_target_pairs={{0,12},{1,13},{2,14},{3,15},{4,8},{5,9},{6,10},{7,11},{8,4},{9,5},... | collective-permute-start | bytes 294920 | tf_op jit(solution)/shard_map/ppermute | solution.py:357
  152.7 0.8 collective-permute-start.7
  153.5 2.9 %all-to-all-done.1 = bf16[32,2,256]{2,1,0:T(2,128)(2,1)S(1)} async-done(((bf16[32,2,256]{2,1,0:T(2,128)(2,1)}), bf16[32,2,256]{2,1,0:T(2,128)(2,1)S(1)}, u32[]{:S(2)}, u32[]{:S(2)}) %all-to-all-start.1) | async-done | bytes 32800 | tf_op jit(solution)/shard_map/all_to_all | solution.py:361
  156.5 1.2 convolution_bitcast_fusion
  157.8 4.2 %collective-permute-done.8 = bf16[64,768]{1,0:T(8,128)(2,1)S(1)} collective-permute-done((bf16[64,768]{1,0:T(8,128)(2,1)S(1)}, bf16[64,768]{1,0:T(8,128)(2,1)S(1)}, u32[]{:S(2)}, u32[]{:S(2)}) %collective-permute-start.8) | collective-permute-done | bytes 98336 | tf_op jit(solution)/shard_map/ppermute | solution.py:357
  (38 shorter events, 4.6 us)
Async XLA Ops:
  0.6 1.0 copy-start
  0.6 13.3 %copy-start.3 = (s32[4096]{0:T(1024)S(1)}, s32[4096]{0:T(1024)}, u32[]{:S(2)}) copy-start(s32[4096]{0:T(1024)} %param.8) | copy-start | bytes 49156
  3.8 14.0 %all-to-all-start = ((bf16[16,8,128]{2,1,0:T(8,128)(2,1)}), bf16[16,8,128]{2,1,0:T(8,128)(2,1)S(1)}, u32[]{:S(2)}, u32[]{:S(2)}) async-start(bf16[16,8,128]{2,1,0:T(8,128)(2,1)} %bitcast.2), calls=%async_computation | async-start | bytes 65536 | tf_op jit(solution)/shard_map/all_to_all | solution.py:191
  12.4 19.9 %collective-permute-start = (bf16[1,512,768]{2,1,0:T(8,128)(2,1)S(1)}, bf16[1,512,768]{2,1,0:T(8,128)(2,1)S(1)}, u32[]{:S(2)}, u32[]{:S(2)}) collective-permute-start(bf16[1,512,768]{2,1,0:T(8,128)(2,1)S(1)} %dynamic-slice_bitcast_fusion), channel_id=1, source_target_pairs={{0,16},{16,0},{1,17},{17,1},{2,18},{18,2},{3,19},{19,3},{4,20},{20... | collective-permute-start | bytes 2359304 | tf_op jit(solution)/shard_map/ppermute | solution.py:160
  32.3 15.6 %copy-start.5 = (bf16[1,512,768]{2,1,0:T(8,128)(2,1)}, bf16[1,512,768]{2,1,0:T(8,128)(2,1)S(1)}, u32[]{:S(2)}) copy-start(bf16[1,512,768]{2,1,0:T(8,128)(2,1)S(1)} %collective-permute-done.mine_ref) | copy-start | bytes 2359300
  32.3 15.6 %collective-permute-start.1 = (bf16[1,512,768]{2,1,0:T(8,128)(2,1)S(1)}, bf16[1,512,768]{2,1,0:T(8,128)(2,1)S(1)}, u32[]{:S(2)}, u32[]{:S(2)}) collective-permute-start(bf16[1,512,768]{2,1,0:T(8,128)(2,1)S(1)} %collective-permute-done.mine_ref), channel_id=1, source_target_pairs={{0,1},{1,0},{2,3},{3,2},{4,5},{5,4},{6,7},{7,6},{8,9},{9,8},{10,11... | collective-permute-start | bytes 2359304 | tf_op jit(solution)/shard_map/ppermute | solution.py:161
  47.9 0.9 copy-start.6
  73.6 4.7 %collective-permute-start.2 = (f32[8,3,512]{2,1,0:T(4,128)}, f32[8,3,512]{2,1,0:T(4,128)S(1)}, u32[]{:S(2)}, u32[]{:S(2)}) collective-permute-start(f32[8,3,512]{2,1,0:T(4,128)} %get-tuple-element.27), channel_id=1, source_target_pairs={{0,16},{16,0},{1,17},{17,1},{2,18},{18,2},{3,19},{19,3},{4,20},{20... | collective-permute-start | bytes 147464 | tf_op jit(solution)/shard_map/ppermute | solution.py:254
  101.2 2.5 %collective-permute-start.3 = (bf16[512,768]{1,0:T(8,128)(2,1)}, bf16[512,768]{1,0:T(8,128)(2,1)S(1)}, u32[]{:S(2)}, u32[]{:S(2)}) collective-permute-start(bf16[512,768]{1,0:T(8,128)(2,1)} %get-tuple-element.32), channel_id=1, source_target_pairs={{0,1},{1,0},{2,3},{3,2},{4,5},{5,4},{6,7},{7,6},{8,9},{9,8},{10,11... | collective-permute-start | bytes 2359304 | tf_op jit(solution)/shard_map/ppermute | solution.py:330
  105.0 25.4 %collective-permute-start.5 = (bf16[512,768]{1,0:T(8,128)(2,1)S(1)}, bf16[512,768]{1,0:T(8,128)(2,1)S(1)}, u32[]{:S(2)}, u32[]{:S(2)}) collective-permute-start(bf16[512,768]{1,0:T(8,128)(2,1)S(1)} %add_convert_fusion.1), channel_id=1, source_target_pairs={{0,16},{16,0},{1,17},{17,1},{2,18},{18,2},{3,19},{19,3},{4,20},{20... | collective-permute-start | bytes 2359304 | tf_op jit(solution)/shard_map/ppermute | solution.py:335
  118.9 11.6 %collective-permute-start.4 = (bf16[512,768]{1,0:T(8,128)(2,1)}, bf16[512,768]{1,0:T(8,128)(2,1)S(1)}, u32[]{:S(2)}, u32[]{:S(2)}) collective-permute-start(bf16[512,768]{1,0:T(8,128)(2,1)} %get-tuple-element.39), channel_id=1, source_target_pairs={{0,1},{1,0},{2,3},{3,2},{4,5},{5,4},{6,7},{7,6},{8,9},{9,8},{10,11... | collective-permute-start | bytes 2359304 | tf_op jit(solution)/shard_map/ppermute | solution.py:330
  119.6 10.9 %copy-start.1 = (bf16[512,768]{1,0:T(8,128)(2,1)S(1)}, bf16[512,768]{1,0:T(8,128)(2,1)}, u32[]{:S(2)}) copy-start(bf16[512,768]{1,0:T(8,128)(2,1)} %get-tuple-element.38) | copy-start | bytes 2359300
  130.8 12.6 %copy-start.2 = (bf16[4,1,2048]{2,1,0:T(2,128)(2,1)S(1)}, bf16[4,1,2048]{2,1,0:T(2,128)(2,1)}, u32[]{:S(2)}) copy-start(bf16[4,1,2048]{2,1,0:T(2,128)(2,1)} %code_grad.2) | copy-start | bytes 49156
  130.8 13.6 %collective-permute-start.6 = (bf16[2,2,64,768]{3,2,1,0:T(8,128)(2,1)S(1)}, bf16[2,2,64,768]{3,2,1,0:T(8,128)(2,1)S(1)}, u32[]{:S(2)}, u32[]{:S(2)}) collective-permute-start(bf16[2,2,64,768]{3,2,1,0:T(8,128)(2,1)S(1)} %dynamic-slice_bitcast_fusion.1), channel_id=1, source_target_pairs={{0,2},{1,3},{2,0},{3,1},{4,6},{5,7},{6,4},{7,5},{8,10},{9,11},{10,... | collective-permute-start | bytes 1179656 | tf_op jit(solution)/shard_map/ppermute | solution.py:169
  143.4 13.1 %copy-start.4 = (s32[128]{0:T(128)S(1)}, s32[128]{0:T(128)}, u32[]{:S(2)}) copy-start(s32[128]{0:T(128)} %param.9) | copy-start | bytes 1540
  145.3 11.1 %all-to-all-start.1 = ((bf16[32,2,256]{2,1,0:T(2,128)(2,1)}), bf16[32,2,256]{2,1,0:T(2,128)(2,1)S(1)}, u32[]{:S(2)}, u32[]{:S(2)}) async-start(bf16[32,2,256]{2,1,0:T(2,128)(2,1)} %reshape.90), calls=%async_computation.1 | async-start | bytes 65536 | tf_op jit(solution)/shard_map/all_to_all | solution.py:361
  149.0 8.7 %collective-permute-start.9 = (bf16[64,768]{1,0:T(8,128)(2,1)S(1)}, bf16[64,768]{1,0:T(8,128)(2,1)S(1)}, u32[]{:S(2)}, u32[]{:S(2)}) collective-permute-start(bf16[64,768]{1,0:T(8,128)(2,1)S(1)} %get-tuple-element.51), channel_id=1, source_target_pairs={{0,12},{1,13},{2,14},{3,15},{4,8},{5,9},{6,10},{7,11},{8,4},{9,5},... | collective-permute-start | bytes 294920 | tf_op jit(solution)/shard_map/ppermute | solution.py:357
  152.7 9.2 %collective-permute-start.8 = (bf16[64,768]{1,0:T(8,128)(2,1)S(1)}, bf16[64,768]{1,0:T(8,128)(2,1)S(1)}, u32[]{:S(2)}, u32[]{:S(2)}) collective-permute-start(bf16[64,768]{1,0:T(8,128)(2,1)S(1)} %get-tuple-element.52), channel_id=1, source_target_pairs={{0,8},{1,9},{2,10},{3,11},{4,12},{5,13},{6,14},{7,15},{8,0},{9,1},... | collective-permute-start | bytes 294920 | tf_op jit(solution)/shard_map/ppermute | solution.py:357
  152.7 9.2 %collective-permute-start.7 = (bf16[64,768]{1,0:T(8,128)(2,1)S(1)}, bf16[64,768]{1,0:T(8,128)(2,1)S(1)}, u32[]{:S(2)}, u32[]{:S(2)}) collective-permute-start(bf16[64,768]{1,0:T(8,128)(2,1)S(1)} %get-tuple-element.50), channel_id=1, source_target_pairs={{0,4},{1,5},{2,6},{3,7},{4,0},{5,1},{6,2},{7,3},{8,12},{9,13},{10,... | collective-permute-start | bytes 294920 | tf_op jit(solution)/shard_map/ppermute | solution.py:357

commit v3 on v2

--- a/solution.py
+++ b/solution.py
@@ -16,11 +16,6 @@
 
 def matmul_cost(m, k, n, nbytes):
     return pl.CostEstimate(flops=2 * m * k * n, bytes_accessed=nbytes, transcendentals=0)
-
-
-def silu_grad(value):
-    sig = jax.nn.sigmoid(value)
-    return sig * (1.0 + value * (1.0 - sig))
 
 
 def code_kernel(classes, act_ref, table_ref, code_ref, slope_ref, half_ref):
@@ -102,15 +97,23 @@
     send_ref[...] = jnp.where(is_first, second, first).astype(jnp.bfloat16)
 
 
-def head_grad_kernel(block, slots, where_ref, p_ref, scale_ref, at_label_ref, label_ref, feat_ref, code_ref, gh_ref, keep_ref, send_ref, all_ref):
+def head_grad_kernel(clients, block, slots, others, where_ref, p_ref, label_ref, stat_ref, *refs):
+    feat_ref, code_ref, gh_ref, keep_ref, send_ref, loss_ref, all_ref = refs[others:]
     step = pl.program_id(0)
     rows = p_ref.shape[0]
 
     @pl.when(step < slots)
     def _():
+        parts = [stat_ref, *refs[:others]]
+        top = functools.reduce(jnp.maximum, [part[0, 0:1, :] for part in parts])
+        total = sum(part[0, 1:2, :] * jnp.exp(part[0, 0:1, :] - top) for part in parts)
+        target = sum(part[0, 2:3, :] for part in parts)
+        loss_ref[0] = top + jnp.log(total) - target
+        scale = jnp.exp(stat_ref[0, 0:1, :] - top) / (total * clients)
+        at_label = (jnp.exp(target - top) / total - 1.0) / clients
         number = lax.broadcasted_iota(jnp.int32, p_ref.shape, 0)
-        grad = p_ref[...].astype(jnp.float32) * scale_ref[0]
-        grad = jnp.where(number == label_ref[0], at_label_ref[0], grad)
+        grad = p_ref[...].astype(jnp.float32) * scale
+        grad = jnp.where(number == label_ref[0], at_label, grad)
         gh = jnp.dot(
             grad.astype(jnp.bfloat16), feat_ref[...], preferred_element_type=jnp.float32
         ).astype(jnp.bfloat16)
@@ -122,7 +125,7 @@
         store_emit_grad(block, where_ref[1] == 0, code_ref[...], all_ref[...], keep_ref, send_ref)
 
 
-def store_code_grad(gh, slope_ref, emit_ref, pre_slope_ref, out_ref):
+def store_code_grad(gh, slope_ref, emit_ref, pre_ref, out_ref):
     hidden = emit_ref.shape[0]
     width = min(512, hidden)
     for c in range(hidden // width):
@@ -132,11 +135,14 @@
         )
         slope = slope_ref[:, cols].astype(jnp.float32)
         grad_sum = 0.5 * jnp.sum(grad_code * slope, axis=0, keepdims=True)
-        out_ref[0, :, cols] = (grad_sum * pre_slope_ref[0, :, cols]).astype(out_ref.dtype)
-
-
-def code_grad_kernel(slope_ref, emit_ref, pre_slope_ref, gh_ref, out_ref):
-    store_code_grad(gh_ref[...], slope_ref, emit_ref, pre_slope_ref, out_ref)
+        v = 0.5 * pre_ref[0, :, cols]
+        th = jnp.tanh(v)
+        pre_slope = 0.5 * (1.0 + th) * (1.0 + v * (1.0 - th))
+        out_ref[0, :, cols] = (grad_sum * pre_slope).astype(out_ref.dtype)
+
+
+def code_grad_kernel(slope_ref, emit_ref, pre_ref, gh_ref, out_ref):
+    store_code_grad(gh_ref[...], slope_ref, emit_ref, pre_ref, out_ref)
 
 
 def emit_grad_kernel(block, where_ref, gh_ref, code_ref, keep_ref, send_ref):
@@ -194,7 +200,6 @@
     pre_own = pre_own.transpose(1, 0, 2).reshape(slots, hidden).astype(f32)
     mine, theirs = gather_emit(emit_source, client_index)
     act = (0.5 * jax.nn.silu(pre_own))[:, None, :]
-    pre_slope = silu_grad(pre_own)[:, None, :]
     local = labels - emit_index * classes
     local = jnp.where((local >= 0) & (local < classes), local, -1).reshape(slots, 1, samples)
 
@@ -249,16 +254,7 @@
         name="forward",
     )(where, code, emit_weight, mine, theirs, features, local)
 
-    top, total, target = stats[:, 0], stats[:, 1], stats[:, 2]
-    for bit in bits_of(emits):
-        other = lax.ppermute(jnp.stack([top, total, target], 1), "emit", xor_pairs(emits, bit))
-        new_top = jnp.maximum(top, other[:, 0])
-        total = total * jnp.exp(top - new_top) + other[:, 1] * jnp.exp(other[:, 0] - new_top)
-        target = target + other[:, 2]
-        top = new_top
-    loss = (top + jnp.log(total) - target).reshape(slots * samples)
-    scale = (jnp.exp(stats[:, 0] - top) / (total * clients))[:, None, :]
-    at_label = ((jnp.exp(target - top) / total - 1.0) / clients)[:, None, :]
+    others = [lax.ppermute(stats, "emit", xor_pairs(emits, j)) for j in range(1, emits)]
 
     block = hidden // (emits * client_size)
     width = min(256, hidden // 2)
@@ -268,28 +264,31 @@
     slot_of = lambda s: jnp.minimum(s, slots - 1)
     step_of = lambda s: jnp.maximum(s - slots, 0)
 
-    gh, keep_a, send_a = pl.pallas_call(
-        functools.partial(head_grad_kernel, block, slots),
+    gh, keep_a, send_a, loss = pl.pallas_call(
+        functools.partial(head_grad_kernel, clients, block, slots, emits - 1),
         grid_spec=pltpu.PrefetchScalarGridSpec(
             num_scalar_prefetch=1,
             grid=(slots + steps,),
             in_specs=[
                 pl.BlockSpec((rows, samples), lambda s, w: (slot_of(s), 0)),
                 pl.BlockSpec((1, 1, samples), lambda s, w: (slot_of(s), 0, 0)),
-                pl.BlockSpec((1, 1, samples), lambda s, w: (slot_of(s), 0, 0)),
-                pl.BlockSpec((1, 1, samples), lambda s, w: (slot_of(s), 0, 0)),
+                *[pl.BlockSpec((1, 3, samples), lambda s, w: (slot_of(s), 0, 0))] * emits,
                 pl.BlockSpec((samples, feat_dim), lambda s, w: (slot_of(s), 0)),
                 pl.BlockSpec((slots * rows, width), lambda s, w: (0, w[0] + step_of(s))),
             ],
             out_specs=[pl.BlockSpec((rows, feat_dim), lambda s, w: (slot_of(s), 0))]
-            + [pl.BlockSpec((width // 2, feat_dim), lambda s, w: (step_of(s), 0))] * 2,
+            + [pl.BlockSpec((width // 2, feat_dim), lambda s, w: (step_of(s), 0))] * 2
+            + [pl.BlockSpec((1, 1, samples), lambda s, w: (slot_of(s), 0, 0))],
             scratch_shapes=[pltpu.VMEM((slots * rows, feat_dim), bf16)],
         ),
-        out_shape=[pltpu.HBM((slots * rows, feat_dim), bf16)] + halves,
+        out_shape=[pltpu.HBM((slots * rows, feat_dim), bf16)]
+        + halves
+        + [jax.ShapeDtypeStruct((slots, 1, samples), f32)],
         compiler_params=params(58),
         cost_estimate=matmul_cost(feat_dim, slots * rows, hidden // 2 + samples, 20 * MIB),
         name="head_grad",
-    )(at(1 - where[2]), p, scale, at_label, local, features, code)
+    )(at(1 - where[2]), p, local, stats, *others, features, code)
+    loss = loss.reshape(slots * samples)
 
     def emit_rest(gh, code):
         return pl.pallas_call(
@@ -324,7 +323,7 @@
             compiler_params=params(58),
             cost_estimate=matmul_cost(count * rows, feat_dim, hidden, 3 * count * MIB),
             name="code_grad",
-        )(slope, emit_full, pre_slope, gh)
+        )(slope, emit_full, pre_own[:, None, :], gh)
 
     add = lambda *terms: sum(t.astype(f32) for t in terms).astype(bf16)
     swap_core = lambda v: lax.ppermute(v, "client", xor_pairs(client_size, 1))

time: 163 us -> 162 us (level)
  other arithmetic: 11.4 us -> 6.64 us
  starting transfers between devices: 21.9 us -> 23.9 us
    ppermute x1, waiting for transfers between devices: 13.6 us -> 4.95 us  [gather_emit(): lax.ppermute(mine, 'emit', xor_pairs(emits, bit))]
    ppermute x1, waiting for transfers between devices: 0.01 us -> 7.16 us  [per_device(): from_pair = lax.ppermute(sum_a, 'emit', xor_pairs(emits, top_bit))]
    div x2 -> x0, other arithmetic: 3.26 us -> none  [the longest x1 1.67 us: per_device(): at_label = ((jnp.exp(target - top) / total - 1.0) / clients)[:, None, :]]
    all_to_all x1, waiting for transfers between devices: 2.56 us -> 5.42 us  [per_device(): lax.all_to_all(pre_slots.reshape(client_size, slots, hidden // client_siz...]
    unnamed x16 -> x20, local copies, waits for them, and re-layouts: 2.77 us -> 3.4 us
  transfers between devices with their start and end apart: 12 -> 12, of which waited for: 6 -> 7; matrix products, arithmetic and copies ran while one was open for 5% -> 4% of each run, Pallas kernels for 30% -> 23%
where the time goes in v3:
time: 162 us; the launch traced here: 161 us
  Pallas kernels  93.5 us (58%)
  waiting for transfers between devices  28.5 us (18%)
  starting transfers between devices  23.9 us (15%)
  other arithmetic  6.64 us (4%)
  local copies, waits for them, and re-layouts  4.83 us (3%)
  matrix products  3.3 us (2%)
    pallas_call x1, Pallas kernels, per_device(): pl.pallas_call(functools.partial(forward_kernel, classes), grid_spec=pltp...  24.9 us
    pallas_call x2, Pallas kernels, code_grad(): pl.pallas_call(code_grad_kernel, grid=(count,), in_specs=[pl.BlockSpec((r...  21.8 us
    pallas_call x1, Pallas kernels, per_device(): pl.pallas_call(functools.partial(head_grad_kernel, clients, block, slots,...  19.8 us
    pallas_call x1, Pallas kernels, per_device(): code, slope = make_code(act, class_table)  14.8 us
    pallas_call x1, Pallas kernels, emit_rest(): pl.pallas_call(functools.partial(emit_grad_kernel, block), grid_spec=pltp...  12.3 us
    ppermute x1, waiting for transfers between devices, per_device(): from_pair = lax.ppermute(sum_a, 'emit', xor_pairs(emits, top_bit))  7.16 us
    all_to_all x1, starting transfers between devices, per_device(): lax.all_to_all(pre_slots.reshape(client_size, slots, hidden // client_siz...  5.91 us
    all_to_all x1, waiting for transfers between devices, per_device(): lax.all_to_all(pre_slots.reshape(client_size, slots, hidden // client_siz...  5.42 us
  transfers between devices with their start and end apart: 12, of which 7 were waited for; matrix products, arithmetic and copies ran while one was open for 4% of the time, Pallas kernels for 23%

profile of v3, /device:TPU:0, one launch (start us, length us, event | category | flops | bytes accessed | tf_op | source)
XLA Modules:
  0.0 161.5 jit_solution(13074976884109092776)
XLA Ops:
  0.7 1.0 copy-done
  1.7 2.1 %convolution_convert_fusion = bf16[128,128]{1,0:T(8,128)(2,1)} fusion(bf16[128,2048]{1,0:T(8,128)(2,1)S(1)} %copy-done, bf16[2048,128]{1,0:T(8,128)(2,1)} %param.11, s32[128]{0:T(128)} %param.9), kind=kOutput, calls=%fused_computation.3 | convolution fusion | flops 71352320 | bytes 1081856 | tf_op jit(solution)/shard_map/dot_general | solution.py:195
  3.8 1.2 dynamic-slice_bitcast_fusion
  4.9 3.1 %collective-permute-start = (bf16[1,512,768]{2,1,0:T(8,128)(2,1)S(1)}, bf16[1,512,768]{2,1,0:T(8,128)(2,1)S(1)}, u32[]{:S(2)}, u32[]{:S(2)}) collective-permute-start(bf16[1,512,768]{2,1,0:T(8,128)(2,1)S(1)} %dynamic-slice_bitcast_fusion), channel_id=1, source_target_pairs={{0,16},{16,0},{1,17},{17,1},{2,18},{18,2},{3,19},{19,3},{4,20},{20... | collective-permute-start | bytes 2359304 | tf_op jit(solution)/shard_map/ppermute | solution.py:166
  8.0 5.9 %all-to-all-start = ((bf16[16,8,128]{2,1,0:T(8,128)(2,1)}), bf16[16,8,128]{2,1,0:T(8,128)(2,1)S(1)}, u32[]{:S(2)}, u32[]{:S(2)}) async-start(bf16[16,8,128]{2,1,0:T(8,128)(2,1)} %bitcast.3), calls=%async_computation | async-start | bytes 65536 | tf_op jit(solution)/shard_map/all_to_all | solution.py:197
  15.1 5.4 %all-to-all-done = bf16[16,8,128]{2,1,0:T(8,128)(2,1)S(1)} async-done(((bf16[16,8,128]{2,1,0:T(8,128)(2,1)}), bf16[16,8,128]{2,1,0:T(8,128)(2,1)S(1)}, u32[]{:S(2)}, u32[]{:S(2)}) %all-to-all-start) | async-done | bytes 32800 | tf_op jit(solution)/shard_map/all_to_all | solution.py:197
  20.6 5.0 %collective-permute-done.mine_ref = bf16[1,512,768]{2,1,0:T(8,128)(2,1)S(1)} collective-permute-done((bf16[1,512,768]{2,1,0:T(8,128)(2,1)S(1)}, bf16[1,512,768]{2,1,0:T(8,128)(2,1)S(1)}, u32[]{:S(2)}, u32[]{:S(2)}) %collective-permute-start) | collective-permute-done | bytes 786464 | tf_op jit(solution)/shard_map/ppermute | solution.py:166
  25.6 0.9 fusion.3.act_ref
  26.4 14.8 %code.1 = (bf16[4096,2048]{1,0:T(8,128)(2,1)}, bf16[4096,2048]{1,0:T(8,128)(2,1)}) custom-call(f32[8,1,2048]{2,1,0:T(1,128)} %fusion.3.act_ref, bf16[500,2048]{1,0:T(8,128)(2,1)} %table_ref.1), custom_call_target="tpu_custom_call" | custom-call | flops 4000000000 | bytes 33554432 | tf_op jit(solution)/shard_map/code/pallas_call | solution.py:225
  41.2 0.9 copy-done.7
  42.1 24.9 %forward.1 = (bf16[4096,512]{1,0:T(8,128)(2,1)}, f32[8,3,512]{2,1,0:T(4,128)}, bf16[2048,768]{1,0:T(8,128)(2,1)}) custom-call(s32[3]{0:T(128)} %pad_add_fusion.1.where_ref, bf16[4096,2048]{1,0:T(8,128)(2,1)} %get-tuple-element.37.code_ref.refs_2_, bf16[1024,768]{1,0:T(8,128)(2,1)} %local_ref.1, bf16[1,512,768]{2,1,0:T(8,128)(2,1)} %copy-done.6, ...), custom_call_target="tpu_custom_call" | custom-call | flops 16106127360 | bytes 31457280 | tf_op jit(solution)/shard_map/forward/pallas_call | solution.py:227
  67.0 1.8 %collective-permute-start.2 = (f32[8,3,512]{2,1,0:T(4,128)}, f32[8,3,512]{2,1,0:T(4,128)S(1)}, u32[]{:S(2)}, u32[]{:S(2)}) collective-permute-start(f32[8,3,512]{2,1,0:T(4,128)} %get-tuple-element.29.stat_ref), channel_id=1, source_target_pairs={{0,16},{16,0},{1,17},{17,1},{2,18},{18,2},{3,19},{19,3},{4,20},{20... | collective-permute-start | bytes 147464 | tf_op jit(solution)/shard_map/ppermute | solution.py:257
  69.4 2.3 %collective-permute-done.2.refs_0_ = f32[8,3,512]{2,1,0:T(4,128)S(1)} collective-permute-done((f32[8,3,512]{2,1,0:T(4,128)}, f32[8,3,512]{2,1,0:T(4,128)S(1)}, u32[]{:S(2)}, u32[]{:S(2)}) %collective-permute-start.2) | collective-permute-done | bytes 49184 | tf_op jit(solution)/shard_map/ppermute | solution.py:257
  71.7 0.6 copy-done.8
  72.3 19.8 %head_grad.1 = (bf16[4096,768]{1,0:T(8,128)(2,1)}, bf16[512,768]{1,0:T(8,128)(2,1)}, bf16[512,768]{1,0:T(8,128)(2,1)}, f32[8,1,512]{2,1,0:T(1,128)}) custom-call(s32[2]{0:T(128)} %pad_add_fusion.where_ref, bf16[4096,512]{1,0:T(8,128)(2,1)} %get-tuple-element.28.p_ref, s32[8,1,512]{2,1,0:T(1,128)} %bitcast.48, f32[8,3,512]{2,1,0:T(4,128)} %get-tuple-element.29.stat_ref, ...), custom_call_target="tpu_custom_call" | custom-call | flops 9663676416 | bytes 20971520 | tf_op jit(solution)/shard_map/head_grad/pallas_call | solution.py:267
  92.8 1.9 %collective-permute-done.3 = bf16[512,768]{1,0:T(8,128)(2,1)S(1)} collective-permute-done((bf16[512,768]{1,0:T(8,128)(2,1)}, bf16[512,768]{1,0:T(8,128)(2,1)S(1)}, u32[]{:S(2)}, u32[]{:S(2)}) %collective-permute-start.3) | collective-permute-done | bytes 786464 | tf_op jit(solution)/shard_map/ppermute | solution.py:329
  94.6 1.3 add_convert_fusion.1
  96.0 12.3 %emit_grad.1 = (bf16[512,768]{1,0:T(8,128)(2,1)}, bf16[512,768]{1,0:T(8,128)(2,1)}) custom-call(s32[2]{0:T(128)} %pad_add_fusion.2.where_ref, bf16[4096,768]{1,0:T(8,128)(2,1)} %get-tuple-element.43.gh_ref, bf16[4096,2048]{1,0:T(8,128)(2,1)} %get-tuple-element.37.code_ref.refs_2_), custom_call_target="tpu_custom_call" | custom-call | flops 6442450944 | bytes 12582912 | tf_op jit(solution)/shard_map/emit_grad/pallas_call | solution.py:294
  108.4 1.7 %collective-permute-start.5 = (bf16[512,768]{1,0:T(8,128)(2,1)S(1)}, bf16[512,768]{1,0:T(8,128)(2,1)S(1)}, u32[]{:S(2)}, u32[]{:S(2)}) collective-permute-start(bf16[512,768]{1,0:T(8,128)(2,1)S(1)} %add_convert_fusion.1), channel_id=1, source_target_pairs={{0,16},{16,0},{1,17},{17,1},{2,18},{18,2},{3,19},{19,3},{4,20},{20... | collective-permute-start | bytes 2359304 | tf_op jit(solution)/shard_map/ppermute | solution.py:334
  110.2 10.9 %code_grad.2 = bf16[4,1,2048]{2,1,0:T(2,128)(2,1)} custom-call(bf16[4096,2048]{1,0:T(8,128)(2,1)} %get-tuple-element.31.slope_ref, bf16[2048,768]{1,0:T(8,128)(2,1)} %get-tuple-element.32.emit_ref, f32[8,1,2048]{2,1,0:T(1,128)} %bitcast.43, bf16[4096,768]{1,0:T(8,128)(2,1)} %get-tuple-element.43.gh_ref), custom_call_target="tpu_custom_call" | custom-call | flops 6442450944 | bytes 12582912 | tf_op jit(solution)/shard_map/code_grad/pallas_call | solution.py:312
  121.1 7.2 %collective-permute-done.5 = bf16[512,768]{1,0:T(8,128)(2,1)S(1)} collective-permute-done((bf16[512,768]{1,0:T(8,128)(2,1)S(1)}, bf16[512,768]{1,0:T(8,128)(2,1)S(1)}, u32[]{:S(2)}, u32[]{:S(2)}) %collective-permute-start.5) | collective-permute-done | bytes 786464 | tf_op jit(solution)/shard_map/ppermute | solution.py:334
  128.6 1.8 %collective-permute-start.6 = (bf16[2,2,64,768]{3,2,1,0:T(8,128)(2,1)S(1)}, bf16[2,2,64,768]{3,2,1,0:T(8,128)(2,1)S(1)}, u32[]{:S(2)}, u32[]{:S(2)}) collective-permute-start(bf16[2,2,64,768]{3,2,1,0:T(8,128)(2,1)S(1)} %dynamic-slice_bitcast_fusion.1), channel_id=1, source_target_pairs={{0,2},{1,3},{2,0},{3,1},{4,6},{5,7},{6,4},{7,5},{8,10},{9,11},{10,... | collective-permute-start | bytes 1179656 | tf_op jit(solution)/shard_map/ppermute | solution.py:175
  130.4 10.9 %code_grad.3 = bf16[4,1,2048]{2,1,0:T(2,128)(2,1)} custom-call(bf16[4096,2048]{1,0:T(8,128)(2,1)} %get-tuple-element.31.slope_ref, bf16[2048,768]{1,0:T(8,128)(2,1)} %get-tuple-element.32.emit_ref, f32[8,1,2048]{2,1,0:T(1,128)} %bitcast.44, bf16[4096,768]{1,0:T(8,128)(2,1)} %get-tuple-element.43.gh_ref), custom_call_target="tpu_custom_call" | custom-call | flops 6442450944 | bytes 12582912 | tf_op jit(solution)/shard_map/code_grad/pallas_call | solution.py:312
  141.2 0.9 maximum_reduce_fusion
  142.4 0.7 reshape.74
  143.2 4.9 %all-to-all-start.1 = ((bf16[32,2,256]{2,1,0:T(2,128)(2,1)}), bf16[32,2,256]{2,1,0:T(2,128)(2,1)S(1)}, u32[]{:S(2)}, u32[]{:S(2)}) async-start(bf16[32,2,256]{2,1,0:T(2,128)(2,1)} %reshape.74), calls=%async_computation.1 | async-start | bytes 65536 | tf_op jit(solution)/shard_map/all_to_all | solution.py:360
  148.1 1.8 %collective-permute-start.7 = (bf16[64,768]{1,0:T(8,128)(2,1)S(1)}, bf16[64,768]{1,0:T(8,128)(2,1)S(1)}, u32[]{:S(2)}, u32[]{:S(2)}) collective-permute-start(bf16[64,768]{1,0:T(8,128)(2,1)S(1)} %get-tuple-element.47), channel_id=1, source_target_pairs={{0,4},{1,5},{2,6},{3,7},{4,0},{5,1},{6,2},{7,3},{8,12},{9,13},{10,... | collective-permute-start | bytes 294920 | tf_op jit(solution)/shard_map/ppermute | solution.py:356
  150.0 2.4 %collective-permute-start.8 = (bf16[64,768]{1,0:T(8,128)(2,1)S(1)}, bf16[64,768]{1,0:T(8,128)(2,1)S(1)}, u32[]{:S(2)}, u32[]{:S(2)}) collective-permute-start(bf16[64,768]{1,0:T(8,128)(2,1)S(1)} %get-tuple-element.49), channel_id=1, source_target_pairs={{0,8},{1,9},{2,10},{3,11},{4,12},{5,13},{6,14},{7,15},{8,0},{9,1},... | collective-permute-start | bytes 294920 | tf_op jit(solution)/shard_map/ppermute | solution.py:356
  152.6 2.9 %all-to-all-done.1 = bf16[32,2,256]{2,1,0:T(2,128)(2,1)S(1)} async-done(((bf16[32,2,256]{2,1,0:T(2,128)(2,1)}), bf16[32,2,256]{2,1,0:T(2,128)(2,1)S(1)}, u32[]{:S(2)}, u32[]{:S(2)}) %all-to-all-start.1) | async-done | bytes 32800 | tf_op jit(solution)/shard_map/all_to_all | solution.py:360
  155.7 1.2 convolution_bitcast_fusion
  156.9 3.9 %collective-permute-done.8 = bf16[64,768]{1,0:T(8,128)(2,1)S(1)} collective-permute-done((bf16[64,768]{1,0:T(8,128)(2,1)S(1)}, bf16[64,768]{1,0:T(8,128)(2,1)S(1)}, u32[]{:S(2)}, u32[]{:S(2)}) %collective-permute-start.8) | collective-permute-done | bytes 98336 | tf_op jit(solution)/shard_map/ppermute | solution.py:356
  160.7 0.7 fusion.2
  (38 shorter events, 3.6 us)
Async XLA Ops:
  0.6 1.0 copy-start
  0.6 13.3 %copy-start.4 = (s32[4096]{0:T(1024)S(1)}, s32[4096]{0:T(1024)}, u32[]{:S(2)}) copy-start(s32[4096]{0:T(1024)} %param.8) | copy-start | bytes 49156
  4.9 20.6 %collective-permute-start = (bf16[1,512,768]{2,1,0:T(8,128)(2,1)S(1)}, bf16[1,512,768]{2,1,0:T(8,128)(2,1)S(1)}, u32[]{:S(2)}, u32[]{:S(2)}) collective-permute-start(bf16[1,512,768]{2,1,0:T(8,128)(2,1)S(1)} %dynamic-slice_bitcast_fusion), channel_id=1, source_target_pairs={{0,16},{16,0},{1,17},{17,1},{2,18},{18,2},{3,19},{19,3},{4,20},{20... | collective-permute-start | bytes 2359304 | tf_op jit(solution)/shard_map/ppermute | solution.py:166
  8.0 12.6 %all-to-all-start = ((bf16[16,8,128]{2,1,0:T(8,128)(2,1)}), bf16[16,8,128]{2,1,0:T(8,128)(2,1)S(1)}, u32[]{:S(2)}, u32[]{:S(2)}) async-start(bf16[16,8,128]{2,1,0:T(8,128)(2,1)} %bitcast.3), calls=%async_computation | async-start | bytes 65536 | tf_op jit(solution)/shard_map/all_to_all | solution.py:197
  20.6 20.6 %copy-start.1 = (f32[8,16,128]{2,1,0:T(8,128)}, f32[8,16,128]{2,1,0:T(8,128)S(1)}, u32[]{:S(2)}) copy-start(f32[8,16,128]{2,1,0:T(8,128)S(1)} %copy.15) | copy-start | bytes 196612
  25.6 15.7 %copy-start.6 = (bf16[1,512,768]{2,1,0:T(8,128)(2,1)}, bf16[1,512,768]{2,1,0:T(8,128)(2,1)S(1)}, u32[]{:S(2)}) copy-start(bf16[1,512,768]{2,1,0:T(8,128)(2,1)S(1)} %collective-permute-done.mine_ref) | copy-start | bytes 2359300
  25.6 15.7 %collective-permute-start.1 = (bf16[1,512,768]{2,1,0:T(8,128)(2,1)S(1)}, bf16[1,512,768]{2,1,0:T(8,128)(2,1)S(1)}, u32[]{:S(2)}, u32[]{:S(2)}) collective-permute-start(bf16[1,512,768]{2,1,0:T(8,128)(2,1)S(1)} %collective-permute-done.mine_ref), channel_id=1, source_target_pairs={{0,1},{1,0},{2,3},{3,2},{4,5},{5,4},{6,7},{7,6},{8,9},{9,8},{10,11... | collective-permute-start | bytes 2359304 | tf_op jit(solution)/shard_map/ppermute | solution.py:167
  41.2 0.9 copy-start.7
  67.0 4.7 %collective-permute-start.2 = (f32[8,3,512]{2,1,0:T(4,128)}, f32[8,3,512]{2,1,0:T(4,128)S(1)}, u32[]{:S(2)}, u32[]{:S(2)}) collective-permute-start(f32[8,3,512]{2,1,0:T(4,128)} %get-tuple-element.29.stat_ref), channel_id=1, source_target_pairs={{0,16},{16,0},{1,17},{17,1},{2,18},{18,2},{3,19},{19,3},{4,20},{20... | collective-permute-start | bytes 147464 | tf_op jit(solution)/shard_map/ppermute | solution.py:257
  71.7 0.6 copy-start.8
  92.1 2.6 %collective-permute-start.3 = (bf16[512,768]{1,0:T(8,128)(2,1)}, bf16[512,768]{1,0:T(8,128)(2,1)S(1)}, u32[]{:S(2)}, u32[]{:S(2)}) collective-permute-start(bf16[512,768]{1,0:T(8,128)(2,1)} %get-tuple-element.34), channel_id=1, source_target_pairs={{0,1},{1,0},{2,3},{3,2},{4,5},{5,4},{6,7},{7,6},{8,9},{9,8},{10,11... | collective-permute-start | bytes 2359304 | tf_op jit(solution)/shard_map/ppermute | solution.py:329
  108.3 12.8 %collective-permute-start.4 = (bf16[512,768]{1,0:T(8,128)(2,1)}, bf16[512,768]{1,0:T(8,128)(2,1)S(1)}, u32[]{:S(2)}, u32[]{:S(2)}) collective-permute-start(bf16[512,768]{1,0:T(8,128)(2,1)} %get-tuple-element.41), channel_id=1, source_target_pairs={{0,1},{1,0},{2,3},{3,2},{4,5},{5,4},{6,7},{7,6},{8,9},{9,8},{10,11... | collective-permute-start | bytes 2359304 | tf_op jit(solution)/shard_map/ppermute | solution.py:329
  108.4 19.8 %collective-permute-start.5 = (bf16[512,768]{1,0:T(8,128)(2,1)S(1)}, bf16[512,768]{1,0:T(8,128)(2,1)S(1)}, u32[]{:S(2)}, u32[]{:S(2)}) collective-permute-start(bf16[512,768]{1,0:T(8,128)(2,1)S(1)} %add_convert_fusion.1), channel_id=1, source_target_pairs={{0,16},{16,0},{1,17},{17,1},{2,18},{18,2},{3,19},{19,3},{4,20},{20... | collective-permute-start | bytes 2359304 | tf_op jit(solution)/shard_map/ppermute | solution.py:334
  110.1 18.1 %copy-start.2 = (bf16[512,768]{1,0:T(8,128)(2,1)S(1)}, bf16[512,768]{1,0:T(8,128)(2,1)}, u32[]{:S(2)}) copy-start(bf16[512,768]{1,0:T(8,128)(2,1)} %get-tuple-element.40) | copy-start | bytes 2359300
  128.6 12.7 %copy-start.3 = (bf16[4,1,2048]{2,1,0:T(2,128)(2,1)S(1)}, bf16[4,1,2048]{2,1,0:T(2,128)(2,1)}, u32[]{:S(2)}) copy-start(bf16[4,1,2048]{2,1,0:T(2,128)(2,1)} %code_grad.2) | copy-start | bytes 49156
  128.6 13.7 %collective-permute-start.6 = (bf16[2,2,64,768]{3,2,1,0:T(8,128)(2,1)S(1)}, bf16[2,2,64,768]{3,2,1,0:T(8,128)(2,1)S(1)}, u32[]{:S(2)}, u32[]{:S(2)}) collective-permute-start(bf16[2,2,64,768]{3,2,1,0:T(8,128)(2,1)S(1)} %dynamic-slice_bitcast_fusion.1), channel_id=1, source_target_pairs={{0,2},{1,3},{2,0},{3,1},{4,6},{5,7},{6,4},{7,5},{8,10},{9,11},{10,... | collective-permute-start | bytes 1179656 | tf_op jit(solution)/shard_map/ppermute | solution.py:175
  141.2 14.4 %copy-start.5 = (s32[128]{0:T(128)S(1)}, s32[128]{0:T(128)}, u32[]{:S(2)}) copy-start(s32[128]{0:T(128)} %param.9) | copy-start | bytes 1540
  143.2 12.3 %all-to-all-start.1 = ((bf16[32,2,256]{2,1,0:T(2,128)(2,1)}), bf16[32,2,256]{2,1,0:T(2,128)(2,1)S(1)}, u32[]{:S(2)}, u32[]{:S(2)}) async-start(bf16[32,2,256]{2,1,0:T(2,128)(2,1)} %reshape.74), calls=%async_computation.1 | async-start | bytes 65536 | tf_op jit(solution)/shard_map/all_to_all | solution.py:360
  148.1 8.7 %collective-permute-start.7 = (bf16[64,768]{1,0:T(8,128)(2,1)S(1)}, bf16[64,768]{1,0:T(8,128)(2,1)S(1)}, u32[]{:S(2)}, u32[]{:S(2)}) collective-permute-start(bf16[64,768]{1,0:T(8,128)(2,1)S(1)} %get-tuple-element.47), channel_id=1, source_target_pairs={{0,4},{1,5},{2,6},{3,7},{4,0},{5,1},{6,2},{7,3},{8,12},{9,13},{10,... | collective-permute-start | bytes 294920 | tf_op jit(solution)/shard_map/ppermute | solution.py:356
  150.0 10.8 %collective-permute-start.8 = (bf16[64,768]{1,0:T(8,128)(2,1)S(1)}, bf16[64,768]{1,0:T(8,128)(2,1)S(1)}, u32[]{:S(2)}, u32[]{:S(2)}) collective-permute-start(bf16[64,768]{1,0:T(8,128)(2,1)S(1)} %get-tuple-element.49), channel_id=1, source_target_pairs={{0,8},{1,9},{2,10},{3,11},{4,12},{5,13},{6,14},{7,15},{8,0},{9,1},... | collective-permute-start | bytes 294920 | tf_op jit(solution)/shard_map/ppermute | solution.py:356
  152.4 8.4 %collective-permute-start.9 = (bf16[64,768]{1,0:T(8,128)(2,1)S(1)}, bf16[64,768]{1,0:T(8,128)(2,1)S(1)}, u32[]{:S(2)}, u32[]{:S(2)}) collective-permute-start(bf16[64,768]{1,0:T(8,128)(2,1)S(1)} %get-tuple-element.48), channel_id=1, source_target_pairs={{0,12},{1,13},{2,14},{3,15},{4,8},{5,9},{6,10},{7,11},{8,4},{9,5},... | collective-permute-start | bytes 294920 | tf_op jit(solution)/shard_map/ppermute | solution.py:356
